TPU v7x, 32 devices: a whole 2x2x4 slice. The times are simulated.
32 devices in a mesh: gx: 4 (over x, core), gy: 2 (over y), gz: 4 (over z).
Axes of the slice: x: 2, y: 2, z: 4, core: 2. Of those that a mesh axis runs over, the one named last changes fastest.
Arguments:
- grid_inputs: bfloat16 [186, 256, 256], P(None, 'gx', 'gy'), may hold values from -6 to 6
- embed_w1: bfloat16 [512, 186], replicated, may hold values from -0.4375 to 0.4375
- embed_b1: float32 [512], replicated, may hold values from -3 to 3
- embed_w2: bfloat16 [512, 512], replicated, may hold values from -0.25 to 0.25
- embed_gain: float32 [512], replicated, may hold values from 0.1 to 1.9
- edge_w1: bfloat16 [512, 1536], replicated, may hold values from -0.15625 to 0.15625
- edge_b1: float32 [512], replicated, may hold values from -3 to 3
- edge_w2: bfloat16 [512, 512], replicated, may hold values from -0.25 to 0.25
- message_gain: float32 [512], replicated, may hold values from 0.1 to 1.9
- message_bias: float32 [512], replicated, may hold values from -3 to 3
- mesh_latent: bfloat16 [512, 4, 2, 256], P('gz', 'gx', 'gy'), may hold values from -6 to 6
- edge_latent: bfloat16 [512, 4, 2, 2048], P('gz', 'gx', 'gy'), may hold values from -6 to 6
- senders: int32 [4, 2, 2048], P('gx', 'gy'), may hold values from 0 to 65535, as said below
- receivers: int32 [4, 2, 2048], P('gx', 'gy'), may hold values from 0 to 2047, as said below
- edge_counts: int32 [4, 2], P('gx', 'gy'), may hold values from 1 to 2048, as said below
Outputs:
- mesh_out: bfloat16 [512, 4, 2, 256], P('gz', 'gx', 'gy')
- grid_latent: bfloat16 [512, 256, 256], P('gz', 'gx', 'gy')
Inputs may be any that keep to these rules, and one draw needn't show every extreme that they name: `senders`: an edge of tile (b, c) has its sender's row within 8 rows of rows b * 64 to (b + 1) * 64 - 1, clipped to the grid, and its column within 8 columns, cyclically, of columns c * 128 to (c + 1) * 128 - 1; this holds in every slot. `receivers`: an edge of tile t is received by a node of that tile, t * 256 to (t + 1) * 256 - 1, in every slot. `edge_counts`: the live edges of a tile are its first slots; some tile holds 2048 live edges.
All inputs are finite; a program needn't handle non-finite values.
Results may differ from a plain program's by a relative error of at most 0.0049.
Values may be sent and summed in bfloat16 or wider, within the bound.
A program may use at most 128 MiB of HBM per device.

v0:
```python
import jax
import jax.numpy as jnp
from jax import lax
from jax.sharding import PartitionSpec as P

HALO = 8
BLOCK = 512


epsilon = 1e-05


def padded_2(value, sides, width):
    for axis, dim in sides:
        size, length = (lax.axis_size(axis), value.shape[dim])
        up = [(i, (i + 1) % size) for i in range(size)]
        down = [(j, i) for i, j in up]
        last = lax.slice_in_dim(value, length - width, length, axis=dim)
        first = lax.slice_in_dim(value, 0, width, axis=dim)
        before = lax.ppermute(last, axis, up)
        after = lax.ppermute(first, axis, down)
        value = jnp.concatenate([before, value, after], axis=dim)
    return value


def normalize(values):
    average = jnp.mean(values, axis=0, keepdims=True)
    centred = values - average
    spread = jnp.mean(centred * centred, axis=0, keepdims=True)
    return centred * lax.rsqrt(spread + epsilon)


def embed_cells(flat_inputs, embed_w1, embed_b1, embed_w2, embed_gain):
    grid_hidden = jax.nn.silu(
        jnp.dot(embed_w1, flat_inputs, preferred_element_type=jnp.float32) + embed_b1[:, None]
    ).astype(jnp.bfloat16)
    grid_pre = jnp.dot(embed_w2, grid_hidden, preferred_element_type=jnp.float32)
    return (normalize(grid_pre) * embed_gain[:, None]).astype(jnp.bfloat16)


def lookup_onehot(mesh_pick, live_mask, node_count):
    node_ids = jnp.arange(node_count, dtype=jnp.int32)
    return ((mesh_pick[:, None] == node_ids[None, :]) & live_mask[:, None]).astype(jnp.bfloat16)


def first_layer(weight_rows, bias_rows, edge_block, grid_cols, mesh_cols, latent):
    first_pre = jnp.dot(weight_rows[:, :latent], edge_block, preferred_element_type=jnp.float32)
    first_pre = first_pre + jnp.dot(
        weight_rows[:, latent : 2 * latent], grid_cols, preferred_element_type=jnp.float32
    )
    first_pre = first_pre + jnp.dot(
        weight_rows[:, 2 * latent :], mesh_cols, preferred_element_type=jnp.float32
    )
    return jax.nn.silu(first_pre + bias_rows[:, None]).astype(jnp.bfloat16)


def on_device(
    grid_inputs,
    embed_w1,
    embed_b1,
    embed_w2,
    embed_gain,
    edge_w1,
    edge_b1,
    edge_w2,
    message_gain,
    message_bias,
    mesh_latent,
    edge_latent,
    senders,
    receivers,
    edge_counts,
):
    latent = embed_w2.shape[0]
    channel_count = grid_inputs.shape[0]
    shard_rows = mesh_latent.shape[0]
    lat_rows = grid_inputs.shape[1]
    lon_cols = grid_inputs.shape[2]
    cell_count = lat_rows * lon_cols
    node_count = mesh_latent.shape[3]
    slot_count = edge_latent.shape[3]
    layer_size = lax.axis_size("gz")
    layer_index = lax.axis_index("gz")
    band_index = lax.axis_index("gx")
    sector = lax.axis_index("gy")
    lon_total = lon_cols * lax.axis_size("gy")
    live_count = edge_counts[0, 0]
    padded_cells = (lat_rows + 2 * HALO) * (lon_cols + 2 * HALO)
    row_start = layer_index * shard_rows
    own_latent = embed_cells(
        grid_inputs.reshape(channel_count, cell_count), embed_w1, embed_b1, embed_w2, embed_gain
    ).reshape(latent, lat_rows, lon_cols)
    padded = padded_2(own_latent, (("gx", 1), ("gy", 2)), HALO)
    pad_flat = padded.reshape(latent, padded_cells)
    grid_out = lax.dynamic_slice_in_dim(own_latent, row_start, shard_rows, 0)
    send_all = senders[0, 0]
    lat_local = send_all // lon_total - band_index * lat_rows + HALO
    lon_local = (send_all % lon_total - sector * lon_cols + HALO + lon_total) % lon_total
    grid_index = lat_local * (lon_cols + 2 * HALO) + lon_local
    tile_index = band_index * lax.axis_size("gy") + sector
    near_index = receivers[0, 0] - tile_index * node_count
    slot_ids = jnp.arange(slot_count, dtype=jnp.int32)
    live_all = slot_ids < live_count
    node_ids = jnp.arange(node_count, dtype=jnp.int32)
    degree = jnp.sum(
        ((near_index[:, None] == node_ids[None, :]) & live_all[:, None]).astype(jnp.int32), axis=0
    )
    mesh_own = mesh_latent[:, 0, 0, :]
    edge_own = edge_latent[:, 0, 0, :]
    lead_size, tail_size = (1, slot_count // layer_size)
    arranged = edge_own.reshape(shard_rows, lead_size, layer_size, tail_size)
    assigned = lax.all_to_all(arranged, "gz", split_axis=2, concat_axis=0, tiled=True).reshape(
        latent, lead_size * tail_size
    )
    mesh_full = lax.all_gather(mesh_own, "gz", axis=0, tiled=True)
    lead_ids = jnp.arange(lead_size, dtype=jnp.int32)[:, None]
    tail_ids = jnp.arange(tail_size, dtype=jnp.int32)[None, :]
    my_slots = ((lead_ids * layer_size + layer_index) * tail_size + tail_ids).reshape(
        lead_size * tail_size
    )
    my_grid = jnp.take(grid_index, my_slots)
    my_near = jnp.take(near_index, my_slots)
    block_starts = my_slots.reshape(-1, BLOCK)[:, 0]
    live_blocks = jnp.sum((block_starts < live_count).astype(jnp.int32))

    def advance_full(block_index, totals):
        live_mask = my_slots < live_count
        onehot = lookup_onehot(my_near, live_mask, node_count)
        grid_cols = jnp.take(pad_flat, my_grid, axis=1)
        mesh_cols = lax.dot_general(
            mesh_full, onehot, (((1,), (1,)), ((), ())), preferred_element_type=jnp.float32
        ).astype(jnp.bfloat16)
        hidden = first_layer(edge_w1, edge_b1, assigned, grid_cols, mesh_cols, latent)
        second = jnp.dot(edge_w2, hidden, preferred_element_type=jnp.float32)
        message = (
            assigned.astype(jnp.float32)
            + normalize(second) * message_gain[:, None]
            + message_bias[:, None]
        ).astype(jnp.bfloat16)
        return totals + jnp.dot(message, onehot, preferred_element_type=jnp.float32)

    partial_totals = lax.fori_loop(
        0, live_blocks, advance_full, jnp.zeros((latent, node_count), jnp.float32)
    )
    totals_own = lax.psum_scatter(partial_totals, "gz", scatter_dimension=0, tiled=True)
    scale = jnp.maximum(degree, 1).astype(jnp.float32)
    result = mesh_own.astype(jnp.float32) + totals_own / scale[None, :]
    return (result.astype(jnp.bfloat16).reshape(shard_rows, 1, 1, node_count), grid_out)


def solution(mesh):
    return jax.shard_map(
        on_device,
        mesh=mesh,
        in_specs=(
            P(None, "gx", "gy"),
            P(),
            P(),
            P(),
            P(),
            P(),
            P(),
            P(),
            P(),
            P(),
            P("gz", "gx", "gy", None),
            P("gz", "gx", "gy", None),
            P("gx", "gy", None),
            P("gx", "gy", None),
            P("gx", "gy"),
        ),
        out_specs=(P("gz", "gx", "gy", None), P("gz", "gx", "gy")),
        check_vma=False,
    )
```

profile of v0, /device:TPU:0, one launch (start us, length us, event | category | flops | bytes accessed | tf_op | source)
XLA Modules:
  0.0 167.0 jit_solution(14069486740867200254)
XLA Ops:
  7.2 0.0 copy-start
  7.2 0.0 copy-start.11
  7.2 0.0 copy-start.12
  7.2 2.6 %pad.17 = bf16[192,64,128]{2,1,0:T(8,128)(2,1)S(1)} pad(bf16[186,64,128]{2,1,0:T(8,128)(2,1)} %param.19, bf16[]{:T(256)} %constant.179), padding=0_6x0_0x0_0 | pad | bytes 6193154
  9.8 4.5 %copy.41 = bf16[24,8,64,128]{3,1,2,0:T(8,128)(2,1)} copy(bf16[24,8,64,128]{3,2,1,0:T(8,128)(2,1)S(1)} %bitcast.63) | data formatting | bytes 6291456
  14.3 0.0 copy-done
  14.3 0.0 copy-done.11
  14.3 0.0 copy-done.12
  14.3 14.6 %fusion.47 = (f32[8192]{0:T(1024)S(1)}, f32[8192,512]{1,0:T(8,128)}) fusion(bf16[512,512]{1,0:T(8,128)(2,1)S(1)} %copy-done, bf16[512,186]{0,1:T(8,128)(2,1)S(1)} %copy-done.11, bf16[186,8192]{1,0:T(8,128)(2,1)} %bitcast.64, f32[512]{0:T(512)S(1)} %copy-done.12), kind=kOutput, calls=%fused_computation.85 | convolution fusion | flops 5884600320 | bytes 20574208 | tf_op jit(solution)/shard_map/dot_general | solution.py:37
  28.9 0.0 copy-start.3
  28.9 0.0 copy-start.10
  28.9 8.6 %multiply_reduce_fusion = f32[8192]{0:T(1024)S(1)} fusion(f32[8192,512]{1,0:T(8,128)} %get-tuple-element.407, f32[8192]{0:T(1024)S(1)} %broadcast_multiply_fusion), kind=kLoop, calls=%fused_computation.4 | loop fusion | flops 12574720 | bytes 16842752 | tf_op jit(solution)/shard_map/reduce_sum | solution.py:29
  37.6 2.0 %copy-done.3 = f32[8192,512]{1,0:T(8,128)S(1)} copy-done((f32[8192,512]{1,0:T(8,128)S(1)}, f32[8192,512]{1,0:T(8,128)}, u32[]{:S(2)}) %copy-start.3) | copy-done | bytes 16777240
  39.6 0.0 copy-done.10
  39.6 4.5 %multiply_convert_fusion = bf16[8192,512]{1,0:T(8,128)(2,1)S(1)} fusion(f32[8192,512]{1,0:T(8,128)S(1)} %copy-done.3, f32[512]{0:T(512)S(1)} %copy-done.10, f32[8192]{0:T(1024)S(1)} %add_rsqrt_fusion, f32[8192]{0:T(1024)S(1)} %broadcast_multiply_fusion), kind=kLoop, calls=%fused_computation.3 | loop fusion | flops 16777216 | bytes 25233408 | tf_op jit(solution)/shard_map/convert_element_type | solution.py:38
  44.1 0.0 copy-start.2
  44.1 0.0 copy-start.7
  44.1 3.2 %copy-done.2 = bf16[8192,512]{1,0:T(8,128)(2,1)} copy-done((bf16[8192,512]{1,0:T(8,128)(2,1)}, bf16[8192,512]{1,0:T(8,128)(2,1)S(1)}, u32[]{:S(2)}) %copy-start.2) | copy-done | bytes 8388632
  47.3 1.5 fusion.46
  48.8 0.5 collective-permute-start
  49.3 1.9 %collective-permute-start.1 = (bf16[512,8,128]{0,2,1:T(8,128)(2,1)}, bf16[512,8,128]{0,2,1:T(8,128)(2,1)S(1)}, u32[]{:S(2)}, u32[]{:S(2)}) collective-permute-start(bf16[512,8,128]{0,2,1:T(8,128)(2,1)} %get-tuple-element.405), channel_id=1, source_target_pairs={{8,0},{16,8},{24,16},{0,24},{9,1},{17,9},{25,17},{1,25},{10,2},{18... | collective-permute-start | bytes 3145736 | tf_op jit(solution)/shard_map/ppermute | solution.py:21
  51.2 0.0 copy-done.6
  51.2 0.3 copy.33
  51.5 1.0 copy.34
  52.5 5.7 %all-to-all-start = ((bf16[128,1,4,512]{3,0,1,2:T(8,128)(2,1)}), bf16[128,1,4,512]{3,0,1,2:T(8,128)(2,1)S(1)}, u32[]{:S(2)}, u32[]{:S(2)}) async-start(bf16[128,1,4,512]{3,0,1,2:T(8,128)(2,1)} %copy.34), calls=%async_computation | async-start | bytes 1048576 | tf_op jit(solution)/shard_map/all_to_all | solution.py:112
  58.2 0.0 reduce-scatter.2.cloned.1.call-start
  58.9 0.0 copy-done.8
  58.9 3.1 %gather_fusion.1 = s32[512]{0:T(512)S(1)} fusion(s32[2048]{0:T(1024)S(1)} %fusion.37, s32[1024]{0:T(1024)S(1)} %pad_clamp_fusion.1), kind=kCustom, calls=%fused_computation.clone | custom fusion | bytes 6144 | tf_op jit(solution)/shard_map/jit(_take)/gather | solution.py:121
  62.1 0.0 copy-done.9
  62.1 10.4 %collective-permute-done = bf16[512,8,128]{0,2,1:T(8,128)(2,1)S(1)} collective-permute-done((bf16[512,8,128]{0,2,1:T(8,128)(2,1)}, bf16[512,8,128]{0,2,1:T(8,128)(2,1)S(1)}, u32[]{:S(2)}, u32[]{:S(2)}) %collective-permute-start) | collective-permute-done | bytes 1048608 | tf_op jit(solution)/shard_map/ppermute | solution.py:20
  72.6 2.5 %collective-permute-done.1 = bf16[512,8,128]{0,2,1:T(8,128)(2,1)S(1)} collective-permute-done((bf16[512,8,128]{0,2,1:T(8,128)(2,1)}, bf16[512,8,128]{0,2,1:T(8,128)(2,1)S(1)}, u32[]{:S(2)}, u32[]{:S(2)}) %collective-permute-start.1) | collective-permute-done | bytes 1048608 | tf_op jit(solution)/shard_map/ppermute | solution.py:21
  75.1 2.4 %pad_maximum_fusion.3 = (bf16[512,80,8]{0,2,1:T(8,128)(2,1)}, bf16[512,80,8]{0,2,1:T(8,128)(2,1)}) fusion(bf16[512,8,128]{0,2,1:T(8,128)(2,1)S(1)} %collective-permute-done.1, bf16[512,64,128]{0,2,1:T(8,128)(2,1)} %bitcast.59, bf16[512,8,128]{0,2,1:T(8,128)(2,1)S(1)} %collective-permute-done), kind=kLoop, calls=%fused_computation.24 | loop fusion | flops 3932160 | bytes 11796480 | tf_op jit(solution)/shard_map/slice | solution.py:18
  77.5 1.5 collective-permute-start.2
  79.0 0.5 collective-permute-start.3
  79.5 0.0 copy-done.7
  79.5 14.0 %all-gather = bf16[512,1,1,256]{3,0,2,1:T(8,128)(2,1)S(1)} all-gather(bf16[128,1,1,256]{3,0,2,1:T(8,128)(2,1)S(1)} %copy-done.7), channel_id=2, replica_groups=mesh['gx'=4,'gy'=2,'gz'=4] {'gz'}, dimensions={0}, use_global_device_ids=true | all-gather | bytes 327680 | tf_op jit(solution)/shard_map/all_gather | solution.py:115
  93.5 3.1 %gather_fusion.2 = s32[512]{0:T(512)S(1)} fusion(s32[2048]{0:T(1024)S(1)} %bitcast.56, s32[1024]{0:T(1024)S(1)} %pad_clamp_fusion.1), kind=kCustom, calls=%fused_computation.1.clone | custom fusion | bytes 6144 | tf_op jit(solution)/shard_map/jit(_take)/gather | solution.py:122
  96.7 0.0 all-to-all-done
  96.7 2.5 %fusion.16 = f32[512,512]{1,0:T(8,128)} fusion(bf16[512,512]{1,0:T(8,128)(2,1)S(1)} %bitcast.66, bf16[512,1536]{1,0:T(8,128)(2,1)} %param.24), kind=kOutput, calls=%fused_computation.34 | convolution fusion | flops 268435456 | bytes 2097152 | tf_op jit(solution)/shard_map/while/body/dot_general | solution.py:47
  99.1 0.0 collective-permute-done.2
  99.2 9.8 %collective-permute-done.3 = bf16[512,80,8]{0,2,1:T(8,128)(2,1)} collective-permute-done((bf16[512,80,8]{0,2,1:T(8,128)(2,1)}, bf16[512,80,8]{0,2,1:T(8,128)(2,1)}, u32[]{:S(2)}, u32[]{:S(2)}) %collective-permute-start.3) | collective-permute-done | bytes 655392 | tf_op jit(solution)/shard_map/ppermute | solution.py:21
  108.9 12.1 %pad_maximum_fusion = bf16[512,80,144]{0,2,1:T(8,128)(2,1)} fusion(bf16[512,80,8]{0,2,1:T(8,128)(2,1)} %collective-permute-done.3, bf16[512,8,128]{0,2,1:T(8,128)(2,1)S(1)} %collective-permute-done.1, bf16[512,64,128]{0,2,1:T(8,128)(2,1)} %bitcast.60, bf16[512,8,128]{0,2,1:T(8,128)(2,1)S(1)} %collective-permute-done, ...), kind=kLoop, calls=%fused_computation.6 | loop fusion | flops 58982400 | bytes 23592960 | tf_op jit(solution)/shard_map/concatenate | solution.py:22
  121.1 7.9 %gather_fusion = bf16[512,512]{1,0:T(8,128)(2,1)S(1)} fusion(bf16[512,11520]{0,1:T(8,128)(2,1)} %bitcast.62, s32[1024]{0:T(1024)S(1)} %pad_clamp_fusion), kind=kCustom, calls=%fused_computation.2 | custom fusion | bytes 1050624 | tf_op jit(solution)/shard_map/while/body/jit(_take)/gather | solution.py:129
  129.0 1.9 %fusion.3 = f32[512,512]{1,0:T(8,128)S(1)} fusion(f32[512,512]{1,0:T(8,128)} %fusion.16, bf16[512,512]{1,0:T(8,128)(2,1)S(1)} %gather_fusion, bf16[512,1536]{1,0:T(8,128)(2,1)} %param.24, pred[512]{0:T(512)(128)(4,1)S(1)} %get-tuple-element.400), kind=kOutput, calls=%fused_computation.14 | convolution fusion | flops 268959744 | bytes 3146240 | tf_op jit(solution)/shard_map/while/body/dot_general | solution.py:48
  130.9 0.0 copy-done.13
  130.9 0.0 copy-start.1
  131.0 1.9 %multiply_convert_fusion.2 = bf16[512,512]{1,0:T(8,128)(2,1)S(1)} fusion(f32[512,512]{1,0:T(8,128)S(1)} %fusion.3, f32[512]{0:T(512)S(1)} %copy-done.13, bf16[512,1536]{1,0:T(8,128)(2,1)} %param.24, bf16[512,1,1,256]{3,0,2,1:T(8,128)(2,1)S(1)} %all-gather, s32[512]{0:T(512)S(1)} %broadcast_select_fusion, pred[512]{0:T(512)(128)(4,1)S(1)} %fusion.43), kind=kOutput, calls=%fused_computation.20 | convolution fusion | flops 405012480 | bytes 2363904 | tf_op jit(solution)/shard_map/while/body/dot_general | solution.py:51
  132.9 0.0 copy-done.5
  132.9 0.4 fusion.48
  133.4 0.2 multiply_reduce_fusion.1
  133.6 0.0 copy-done.14
  133.6 0.0 copy-done.15
  133.6 0.6 fusion.7
  134.2 0.1 while.17
  134.2 0.1 add.377
  134.4 0.0 copy-start.4
  134.4 0.8 copy-done.4
  135.2 0.0 reduce-scatter.2.cloned.1.call-update
  135.2 1.7 %constant_dynamic-slice_fusion = bf16[128,64,128]{0,2,1:T(8,128)(2,1)S(1)} fusion(bf16[512,64,128]{0,2,1:T(8,128)(2,1)} %bitcast.61, s32[]{:T(128)S(6)} %select_n.56), kind=kLoop, calls=%fused_computation.81 | loop fusion | bytes 4194308 | tf_op jit(solution)/shard_map/dynamic_slice | solution.py:95
  136.9 2.8 %copy.40 = bf16[128,64,128]{2,1,0:T(8,128)(2,1)} copy(bf16[128,64,128]{0,2,1:T(8,128)(2,1)S(1)} %constant_dynamic-slice_fusion) | data formatting | bytes 4194304
  139.7 1.4 convert_reduce_fusion
  141.1 17.5 %reduce-scatter.2.cloned.1.call-done = f32[128,256]{1,0:T(8,128)} async-done(((f32[512,256]{1,0:T(8,128)}), f32[128,256]{1,0:T(8,128)}) %reduce-scatter.2.cloned.1.call-update) | async-done | bytes 131088 | tf_op jit(solution)/shard_map/reduce_scatter | solution.py:145
  158.6 1.6 fusion.33
  160.1 0.0 copy-done.1
  (23 shorter events, 0.2 us)
Async XLA Ops:
  7.2 7.2 %copy-start = (bf16[512,512]{1,0:T(8,128)(2,1)S(1)}, bf16[512,512]{1,0:T(8,128)(2,1)}, u32[]{:S(2)}) copy-start(bf16[512,512]{1,0:T(8,128)(2,1)} %param.22) | copy-start | bytes 1572868
  7.2 7.1 %copy-start.11 = (bf16[512,186]{0,1:T(8,128)(2,1)S(1)}, bf16[512,186]{0,1:T(8,128)(2,1)}, u32[]{:S(2)}) copy-start(bf16[512,186]{0,1:T(8,128)(2,1)} %param.20) | copy-start | bytes 571396
  7.2 7.1 %copy-start.12 = (f32[512]{0:T(512)S(1)}, f32[512]{0:T(512)}, u32[]{:S(2)}) copy-start(f32[512]{0:T(512)} %param.21) | copy-start | bytes 6148
  28.9 10.7 %copy-start.3 = (f32[8192,512]{1,0:T(8,128)S(1)}, f32[8192,512]{1,0:T(8,128)}, u32[]{:S(2)}) copy-start(f32[8192,512]{1,0:T(8,128)} %get-tuple-element.407) | copy-start | bytes 50331652
  28.9 10.7 %copy-start.10 = (f32[512]{0:T(512)S(1)}, f32[512]{0:T(512)}, u32[]{:S(2)}) copy-start(f32[512]{0:T(512)} %param.23) | copy-start | bytes 6148
  39.6 11.7 %copy-start.6 = (bf16[128,1,1,2048]{3,0,2,1:T(8,128)(2,1)S(1)}, bf16[128,1,1,2048]{3,0,2,1:T(8,128)(2,1)}, u32[]{:S(2)}) copy-start(bf16[128,1,1,2048]{3,0,2,1:T(8,128)(2,1)} %param.30) | copy-start | bytes 1572868
  39.6 19.3 %copy-start.8 = (s32[1,1,2048]{2,1,0:T(1,128)S(1)}, s32[1,1,2048]{2,1,0:T(1,128)}, u32[]{:S(2)}) copy-start(s32[1,1,2048]{2,1,0:T(1,128)} %param.31) | copy-start | bytes 24580
  39.6 22.5 %copy-start.9 = (s32[1,1,2048]{2,1,0:T(1,128)S(1)}, s32[1,1,2048]{2,1,0:T(1,128)}, u32[]{:S(2)}) copy-start(s32[1,1,2048]{2,1,0:T(1,128)} %param.32) | copy-start | bytes 24580
  44.1 3.2 %copy-start.2 = (bf16[8192,512]{1,0:T(8,128)(2,1)}, bf16[8192,512]{1,0:T(8,128)(2,1)S(1)}, u32[]{:S(2)}) copy-start(bf16[8192,512]{1,0:T(8,128)(2,1)S(1)} %multiply_convert_fusion) | copy-start | bytes 25165828
  44.1 35.4 %copy-start.7 = (bf16[128,1,1,256]{3,0,2,1:T(8,128)(2,1)S(1)}, bf16[128,1,1,256]{3,0,2,1:T(8,128)(2,1)}, u32[]{:S(2)}) copy-start(bf16[128,1,1,256]{3,0,2,1:T(8,128)(2,1)} %param.29) | copy-start | bytes 196612
  48.8 23.7 %collective-permute-start = (bf16[512,8,128]{0,2,1:T(8,128)(2,1)}, bf16[512,8,128]{0,2,1:T(8,128)(2,1)S(1)}, u32[]{:S(2)}, u32[]{:S(2)}) collective-permute-start(bf16[512,8,128]{0,2,1:T(8,128)(2,1)} %get-tuple-element.404), channel_id=1, source_target_pairs={{0,8},{8,16},{16,24},{24,0},{1,9},{9,17},{17,25},{25,1},{2,10},{10... | collective-permute-start | bytes 3145736 | tf_op jit(solution)/shard_map/ppermute | solution.py:20
  49.3 25.8 %collective-permute-start.1 = (bf16[512,8,128]{0,2,1:T(8,128)(2,1)}, bf16[512,8,128]{0,2,1:T(8,128)(2,1)S(1)}, u32[]{:S(2)}, u32[]{:S(2)}) collective-permute-start(bf16[512,8,128]{0,2,1:T(8,128)(2,1)} %get-tuple-element.405), channel_id=1, source_target_pairs={{8,0},{16,8},{24,16},{0,24},{9,1},{17,9},{25,17},{1,25},{10,2},{18... | collective-permute-start | bytes 3145736 | tf_op jit(solution)/shard_map/ppermute | solution.py:21
  52.5 44.1 %all-to-all-start = ((bf16[128,1,4,512]{3,0,1,2:T(8,128)(2,1)}), bf16[128,1,4,512]{3,0,1,2:T(8,128)(2,1)S(1)}, u32[]{:S(2)}, u32[]{:S(2)}) async-start(bf16[128,1,4,512]{3,0,1,2:T(8,128)(2,1)} %copy.34), calls=%async_computation | async-start | bytes 1048576 | tf_op jit(solution)/shard_map/all_to_all | solution.py:112
  58.2 100.3 %reduce-scatter.2.cloned.1.call-start = ((), (), s32[]{:S(2)}) async-start(), calls=%async_computation.2 | async-start | bytes 655360 | tf_op jit(solution)/shard_map/reduce_scatter | solution.py:145
  77.5 21.7 %collective-permute-start.2 = (bf16[512,80,8]{0,2,1:T(8,128)(2,1)}, bf16[512,80,8]{0,2,1:T(8,128)(2,1)}, u32[]{:S(2)}, u32[]{:S(2)}) collective-permute-start(bf16[512,80,8]{0,2,1:T(8,128)(2,1)} %get-tuple-element.402), channel_id=1, source_target_pairs={{0,4},{4,0},{1,5},{5,1},{2,6},{6,2},{3,7},{7,3},{8,12},{12,8},{9,1... | collective-permute-start | bytes 1966088 | tf_op jit(solution)/shard_map/ppermute | solution.py:20
  79.0 29.9 %collective-permute-start.3 = (bf16[512,80,8]{0,2,1:T(8,128)(2,1)}, bf16[512,80,8]{0,2,1:T(8,128)(2,1)}, u32[]{:S(2)}, u32[]{:S(2)}) collective-permute-start(bf16[512,80,8]{0,2,1:T(8,128)(2,1)} %get-tuple-element.403), channel_id=1, source_target_pairs={{4,0},{0,4},{5,1},{1,5},{6,2},{2,6},{7,3},{3,7},{12,8},{8,12},{13,... | collective-permute-start | bytes 1966088 | tf_op jit(solution)/shard_map/ppermute | solution.py:21
  99.1 31.8 %copy-start.13 = (f32[512]{0:T(512)S(1)}, f32[512]{0:T(512)}, u32[]{:S(2)}) copy-start(f32[512]{0:T(512)} %param.25) | copy-start | bytes 6148
  121.1 11.9 %copy-start.5 = (bf16[512,512]{1,0:T(8,128)(2,1)S(1)}, bf16[512,512]{1,0:T(8,128)(2,1)}, u32[]{:S(2)}) copy-start(bf16[512,512]{1,0:T(8,128)(2,1)} %param.26) | copy-start | bytes 1572868
  121.1 12.5 %copy-start.14 = (f32[512]{0:T(512)S(1)}, f32[512]{0:T(512)}, u32[]{:S(2)}) copy-start(f32[512]{0:T(512)} %param.28) | copy-start | bytes 6148
  121.1 12.5 %copy-start.15 = (f32[512]{0:T(512)S(1)}, f32[512]{0:T(512)}, u32[]{:S(2)}) copy-start(f32[512]{0:T(512)} %param.27) | copy-start | bytes 6148
  130.9 29.2 %copy-start.1 = (bf16[512,512]{1,0:T(8,128)(2,1)S(1)}, bf16[512,512]{1,0:T(8,128)(2,1)}, u32[]{:S(2)}) copy-start(bf16[512,512]{1,0:T(8,128)(2,1)} %param.22) | copy-start | bytes 1572868
  134.4 0.8 copy-start.4
Sparse Core Ops, SparseCore 0:
  135.3 23.2 reduce-scatter.1
where the time goes:
time: 167 us
  waiting for transfers between devices  40.2 us (24%)
  local copies, waits for them, and re-layouts  34.7 us (21%)
  other arithmetic  31 us (19%)
  matrix products  21.9 us (13%)
  between operations  15 us (9%)
  blocking collectives  14 us (8%)
  starting transfers between devices  10.1 us (6%)
    reduce_scatter x1, waiting for transfers between devices, on_device(): lax.psum_scatter(partial_totals, 'gz', scatter_dimension=0, tiled=True)  17.5 us
    unnamed x36, local copies, waits for them, and re-layouts  16.2 us
    dot_general x1, matrix products, embed_cells(): jnp.dot(embed_w2, grid_hidden, preferred_element_type=jnp.float32)  14.6 us
    all_gather x1, blocking collectives, on_device(): mesh_full = lax.all_gather(mesh_own, 'gz', axis=0, tiled=True)  14 us
    ppermute x2, waiting for transfers between devices, padded_2(): after = lax.ppermute(first, axis, down)  12.3 us
    concatenate x1, other arithmetic, padded_2(): value = jnp.concatenate([before, value, after], axis=dim)  12.1 us
    ppermute x2, waiting for transfers between devices, padded_2(): before = lax.ppermute(last, axis, up)  10.4 us
    reduce_sum x2, other arithmetic, normalize(): spread = jnp.mean(centred * centred, axis=0, keepdims=True)  8.8 us
  transfers between devices with their start and end apart: 6, of which 4 were waited for; matrix products, arithmetic and copies ran while one was open for 11% of the time, Pallas kernels for 0%

commit v1 on v0

v1 whole, which is shorter than its diff:
```python
import functools

import jax
import jax.numpy as jnp
from jax import lax
from jax.experimental import pallas as pl
from jax.experimental.pallas import tpu as pltpu
from jax.sharding import PartitionSpec as P

HALO = 8
ROWS = 16
GROUP = 4

epsilon = 1e-05
F32 = jnp.float32
BF16 = jnp.bfloat16


def shifts(axis):
    size = lax.axis_size(axis)
    up = [(i, (i + 1) % size) for i in range(size)]
    return up, [(j, i) for i, j in up]


def half_silu(half):
    return half + half * jnp.tanh(half)


def centre(values):
    average = jnp.mean(values, axis=0, keepdims=True)
    centred = values - average
    spread = jnp.mean(centred * centred, axis=0, keepdims=True)
    return average, lax.rsqrt(spread + epsilon)


def onehot_of(index_row, first, count):
    ids = lax.broadcasted_iota(jnp.int32, (count, index_row.shape[1]), 0)
    return jnp.where(ids == index_row - first, 1.0, 0.0).astype(BF16)


def embed_kernel(step0, place_ref, x_ref, w1_ref, b1_ref, w2_ref, gain_ref, own_ref, *rest):
    out_ref, gathered_ref, wide, pre_ref, out_wide = rest[-5:]
    channels, rows, lon = x_ref.shape
    padded = w1_ref.shape[1]
    shard = out_ref.shape[0]
    step = pl.program_id(0)

    @pl.when(step == 0)
    def _():
        wide[pl.ds(channels * rows, (padded - channels) * rows), :] = jnp.zeros(
            ((padded - channels) * rows, lon), F32
        )
        if len(rest) == 5:
            gathered_ref[...] = jnp.zeros_like(gathered_ref)
        else:
            gathered_ref[...] = rest[1][...]

    wide[pl.ds(0, channels * rows), :] = x_ref[...].astype(F32).reshape(channels * rows, lon)
    gain = gain_ref[pl.ds(pl.multiple_of(place_ref[0] * shard, shard), shard), :]
    for group in range(rows // GROUP):
        cells = jnp.concatenate(
            [wide[pl.ds(group * GROUP + r, padded, stride=rows), :] for r in range(GROUP)], axis=1
        ).astype(BF16)
        half = jnp.dot(w1_ref[...], cells, preferred_element_type=F32) + b1_ref[...]
        hidden = half_silu(half).astype(BF16)
        pre_ref[...] = jnp.dot(w2_ref[...], hidden, preferred_element_type=F32)
        average, scale = centre(pre_ref[...])
        own = pre_ref[pl.ds(pl.multiple_of(place_ref[0] * shard, shard), shard), :]
        own = (own - average) * scale * gain
        for r in range(GROUP):
            out_wide[pl.ds(group * GROUP + r, shard, stride=rows), :] = own[:, r * lon : (r + 1) * lon]
        first = ((step0 + step) * rows + group * GROUP) * lon
        pick = onehot_of(own_ref[...], first, GROUP * lon)
        gathered_ref[...] += jnp.dot(cells, pick, preferred_element_type=F32)
    out_ref[...] = out_wide[...].reshape(shard, rows, lon).astype(BF16)


def embed(place, inputs, w1, b1, w2, gain, own_index, shard, start, stop, earlier):
    channels, lat, lon = inputs.shape
    latent, padded = w1.shape
    edges = own_index.shape[1]
    steps = (stop - start) // ROWS
    step0 = start // ROWS
    full = lambda a: pl.BlockSpec(a.shape, lambda i: (0,) * a.ndim)
    whole = (latent * padded + latent * latent + padded * edges) * (stop - start) * lon * 2
    return pl.pallas_call(
        functools.partial(embed_kernel, step0),
        grid=(steps,),
        in_specs=[
            pl.BlockSpec(memory_space=pltpu.SMEM),
            pl.BlockSpec((channels, ROWS, lon), lambda i: (0, i + step0, 0)),
            full(w1),
            full(b1),
            full(w2),
            full(gain),
            full(own_index),
        ]
        + ([pl.BlockSpec(memory_space=pl.ANY), full(earlier[1])] if earlier else []),
        out_specs=[
            pl.BlockSpec((shard, ROWS, lon), lambda i: (0, i + step0, 0)),
            pl.BlockSpec((padded, edges), lambda i: (0, 0)),
        ],
        out_shape=[
            jax.ShapeDtypeStruct((shard, lat, lon), BF16),
            jax.ShapeDtypeStruct((padded, edges), F32),
        ],
        scratch_shapes=[
            pltpu.VMEM((padded * ROWS, lon), F32),
            pltpu.VMEM((latent, GROUP * lon), F32),
            pltpu.VMEM((shard * ROWS, lon), F32),
        ],
        input_output_aliases={7: 0} if earlier else {},
        compiler_params=pltpu.CompilerParams(
            dimension_semantics=("arbitrary",), vmem_limit_bytes=40 * 1024 * 1024
        ),
        cost_estimate=pl.CostEstimate(
            flops=whole * 2, bytes_accessed=inputs.size + shard * lat * lon, transcendentals=0
        ),
    )(place, inputs, w1, b1, w2, gain, own_index, *(earlier or ()))


def edge_kernel(
    moved_ref, near_ref, send_ref, gathered_ref, up_ref, down_ref, left_ref, right_ref,
    w1_ref, b1_ref, w2_ref, gain_ref, e1_ref, eb1_ref, e2_ref, mgain_ref, mbias_ref,
    totals_ref, degree_ref,
):
    latent = w2_ref.shape[0]
    edges = send_ref.shape[1]
    slots = near_ref.shape[1]
    nodes = totals_ref.shape[1]
    picked = gathered_ref[...].astype(BF16).astype(F32)[: up_ref.shape[0]]
    first = 0
    for strip in (up_ref, down_ref, left_ref, right_ref):
        count = strip.shape[1]
        pick = onehot_of(send_ref[1:2, :], first, count)
        picked = picked + jnp.dot(strip[...], pick, preferred_element_type=F32)
        first += count
    picked = picked.astype(BF16)
    half = jnp.dot(w1_ref[...], picked, preferred_element_type=F32) + b1_ref[...]
    pre = jnp.dot(w2_ref[...], half_silu(half).astype(BF16), preferred_element_type=F32)
    average, scale = centre(pre)
    sender = ((pre - average) * scale * gain_ref[...]).astype(BF16)
    assigned = moved_ref[:, :edges]
    onehot = onehot_of(send_ref[2:3, :], 0, nodes)
    mesh_cols = jnp.dot(moved_ref[:, edges:], onehot, preferred_element_type=F32).astype(BF16)
    half = jnp.dot(e1_ref[:, :latent], assigned, preferred_element_type=F32)
    half = half + jnp.dot(e1_ref[:, latent : 2 * latent], sender, preferred_element_type=F32)
    half = half + jnp.dot(e1_ref[:, 2 * latent :], mesh_cols, preferred_element_type=F32)
    hidden = half_silu(half + eb1_ref[...]).astype(BF16)
    second = jnp.dot(e2_ref[...], hidden, preferred_element_type=F32)
    average, scale = centre(second)
    message = (
        assigned.astype(F32) + (second - average) * scale * mgain_ref[...] + mbias_ref[...]
    ).astype(BF16)
    last = (((1,), (1,)), ((), ()))
    totals_ref[...] = lax.dot_general(message, onehot, last, preferred_element_type=F32)
    degree = jnp.zeros(degree_ref.shape, F32)
    for start in range(0, slots, edges):
        chunk = onehot_of(near_ref[:, start : start + edges], 0, nodes)
        ones = jnp.ones((degree_ref.shape[0], edges), BF16)
        degree = degree + lax.dot_general(ones, chunk, last, preferred_element_type=F32)
    degree_ref[...] = jnp.maximum(degree, 1.0)


def edge_network(nodes, operands, latent):
    return pl.pallas_call(
        edge_kernel,
        out_shape=[
            jax.ShapeDtypeStruct((latent, nodes), F32),
            jax.ShapeDtypeStruct((8, nodes), F32),
        ],
        compiler_params=pltpu.CompilerParams(vmem_limit_bytes=48 * 1024 * 1024),
        cost_estimate=pl.CostEstimate(
            flops=4_000_000_000, bytes_accessed=8_000_000, transcendentals=0
        ),
    )(*operands)


def on_device(
    grid_inputs,
    embed_w1,
    embed_b1,
    embed_w2,
    embed_gain,
    edge_w1,
    edge_b1,
    edge_w2,
    message_gain,
    message_bias,
    mesh_latent,
    edge_latent,
    senders,
    receivers,
    edge_counts,
):
    latent = embed_w2.shape[0]
    channels, lat, lon = grid_inputs.shape
    shard = mesh_latent.shape[0]
    nodes = mesh_latent.shape[3]
    slots = edge_latent.shape[3]
    layers = lax.axis_size("gz")
    layer = lax.axis_index("gz")
    band = lax.axis_index("gx")
    sector = lax.axis_index("gy")
    lon_total = lon * lax.axis_size("gy")
    share = slots // layers
    padded = -(-channels // 16) * 16

    mesh_own = mesh_latent[:, 0, 0, :]
    edge_own = edge_latent[:, 0, 0, :].reshape(shard, layers, share).transpose(1, 0, 2)
    outgoing = jnp.concatenate(
        [edge_own, jnp.broadcast_to(mesh_own[None], (layers, shard, nodes))], axis=2
    )
    moved = lax.all_to_all(outgoing, "gz", split_axis=0, concat_axis=0, tiled=True)
    moved = moved.reshape(latent, share + nodes)

    up, down = shifts("gx")
    before = lax.ppermute(grid_inputs[:, lat - HALO :, :], "gx", up)
    after = lax.ppermute(grid_inputs[:, :HALO, :], "gx", down)

    slot_ids = jnp.arange(slots, dtype=jnp.int32)
    tile = band * lax.axis_size("gy") + sector
    near = jnp.where(slot_ids < edge_counts[0, 0], receivers[0, 0] - tile * nodes, -1)
    my_near = lax.dynamic_slice_in_dim(near, layer * share, share)
    send = lax.dynamic_slice_in_dim(senders[0, 0], layer * share, share)
    row = send // lon_total - band * lat
    column = (send % lon_total - sector * lon + HALO + lon_total) % lon_total - HALO
    inside_row = (row >= 0) & (row < lat)
    inside_column = (column >= 0) & (column < lon)
    own_index = jnp.where(inside_row & inside_column, row * lon + column, -1)
    strip = HALO * lon
    tall = (lat + 2 * HALO) * HALO
    row_index = jnp.where(row < 0, (row + HALO) * lon, strip + (row - lat) * lon) + column
    column_index = (
        jnp.where(column < 0, column + HALO, tall + column - lon) + 2 * strip + (row + HALO) * HALO
    )
    halo_index = jnp.where(
        inside_column, jnp.where(inside_row, -1, row_index), column_index
    )
    send_table = jnp.stack([own_index, halo_index, my_near])

    pad = lambda w: jnp.pad(w, ((0, 0), (0, padded - channels)))
    half_w1 = embed_w1 * 0.5
    half_b1 = (embed_b1 * 0.5)[:, None]
    gain = embed_gain[:, None]
    place = layer.reshape(1).astype(jnp.int32)
    middle = lat // 2 // ROWS * ROWS
    common = (place, grid_inputs, pad(half_w1), half_b1, embed_w2, gain, send_table[:1], shard)
    partial = embed(*common, 0, middle, None)

    left_cols = jnp.concatenate([a[:, :, :HALO] for a in (before, grid_inputs, after)], axis=1)
    right_cols = jnp.concatenate(
        [a[:, :, lon - HALO :] for a in (before, grid_inputs, after)], axis=1
    )
    up, down = shifts("gy")
    left = lax.ppermute(right_cols.reshape(channels, tall), "gy", up)
    right = lax.ppermute(left_cols.reshape(channels, tall), "gy", down)
    grid_out, gathered = embed(*common, middle, lat, partial)

    totals, degree = edge_network(
        nodes,
        (
            moved, near[None], send_table, gathered,
            before.reshape(channels, strip), after.reshape(channels, strip), left, right,
            half_w1, half_b1, embed_w2, gain,
            edge_w1 * 0.5, (edge_b1 * 0.5)[:, None], edge_w2,
            message_gain[:, None], message_bias[:, None],
        ),
        latent,
    )
    parts = lax.all_to_all(
        totals.reshape(layers, shard, nodes), "gz", split_axis=0, concat_axis=0, tiled=True
    )
    result = mesh_own.astype(F32) + jnp.sum(parts, axis=0) / degree[:1]
    return (result.astype(BF16).reshape(shard, 1, 1, nodes), grid_out)


def solution(mesh):
    return jax.shard_map(
        on_device,
        mesh=mesh,
        in_specs=(
            P(None, "gx", "gy"),
            P(),
            P(),
            P(),
            P(),
            P(),
            P(),
            P(),
            P(),
            P(),
            P("gz", "gx", "gy", None),
            P("gz", "gx", "gy", None),
            P("gx", "gy", None),
            P("gx", "gy", None),
            P("gx", "gy"),
        ),
        out_specs=(P("gz", "gx", "gy", None), P("gz", "gx", "gy")),
        check_vma=False,
    )
```

time: 167 us -> 101 us (0.60)
  Pallas kernels: 0 us -> 24.3 us
  other arithmetic: 31 us -> 8.24 us
  matrix products: 21.9 us -> 0 us
  waiting for transfers between devices: 40.2 us -> 19.2 us
  blocking collectives: 14 us -> 0 us
  between operations: 15 us -> 1.51 us
  starting transfers between devices: 10.1 us -> 14.9 us
  local copies, waits for them, and re-layouts: 34.7 us -> 32.2 us
    pallas_call x0 -> x3, Pallas kernels: none -> 24.3 us  [the longest x2 18.1 us: embed(): pl.pallas_call(functools.partial(embed_kernel, step0), grid=(steps,), in_...]
    dot_general x6 -> x0, matrix products: 21.9 us -> none  [the longest x1 14.6 us: embed_cells(): jnp.dot(embed_w2, grid_hidden, preferred_element_type=jnp.float32)]
    reduce_scatter x1 -> x0, waiting for transfers between devices: 17.5 us -> none  [on_device(): lax.psum_scatter(partial_totals, 'gz', scatter_dimension=0, tiled=True)]
    ppermute x4, waiting for transfers between devices: 22.7 us -> 6.08 us  [the longest x1 3.99 us: on_device(): right = lax.ppermute(left_cols.reshape(channels, tall), 'gy', down)]
    gather x3 -> x0, local copies, waits for them, and re-layouts: 14.2 us -> none  [the longest x1 7.91 us: advance_full(): grid_cols = jnp.take(pad_flat, my_grid, axis=1)]
    all_gather x1 -> x0, blocking collectives: 14 us -> none  [on_device(): mesh_full = lax.all_gather(mesh_own, 'gz', axis=0, tiled=True)]
    all_to_all x1 -> x2, waiting for transfers between devices: 0.01 us -> 13.1 us  [the longest x1 13.1 us: on_device(): lax.all_to_all(totals.reshape(layers, shard, nodes), 'gz', split_axis=0,...]
    concatenate x1, other arithmetic: 12.1 us -> 0.98 us  [on_device(): jnp.concatenate([edge_own, jnp.broadcast_to(mesh_own[None], (layers, shar...]
  transfers between devices with their start and end apart: 6 -> 6, of which waited for: 4 -> 3; matrix products, arithmetic and copies ran while one was open for 11% -> 32% of each run, Pallas kernels for 0% -> 18%
where the time goes in v1:
time: 101 us; the launch traced here: 100 us
  local copies, waits for them, and re-layouts  32.2 us (32%)
  Pallas kernels  24.3 us (24%)
  waiting for transfers between devices  19.2 us (19%)
  starting transfers between devices  14.9 us (15%)
  other arithmetic  8.24 us (8%)
  between operations  1.51 us (1%)
    pallas_call x2, Pallas kernels, embed(): pl.pallas_call(functools.partial(embed_kernel, step0), grid=(steps,), in_...  18.1 us
    unnamed x45, local copies, waits for them, and re-layouts  16.4 us
    all_to_all x1, waiting for transfers between devices, on_device(): lax.all_to_all(totals.reshape(layers, shard, nodes), 'gz', split_axis=0,...  13.1 us
    pallas_call x1, Pallas kernels, edge_network(): pl.pallas_call(edge_kernel, out_shape=[jax.ShapeDtypeStruct((latent, node...  6.2 us
    slice x3, local copies, waits for them, and re-layouts, on_device(): a[:, :, :HALO]  5.71 us
    all_to_all x1, starting transfers between devices, on_device(): lax.all_to_all(outgoing, 'gz', split_axis=0, concat_axis=0, tiled=True)  5.68 us
    all_to_all x1, starting transfers between devices, on_device(): lax.all_to_all(totals.reshape(layers, shard, nodes), 'gz', split_axis=0,...  4.81 us
    ppermute x1, waiting for transfers between devices, on_device(): right = lax.ppermute(left_cols.reshape(channels, tall), 'gy', down)  3.99 us
  transfers between devices with their start and end apart: 6, of which 3 were waited for; matrix products, arithmetic and copies ran while one was open for 32% of the time, Pallas kernels for 18%

profile of v1, /device:TPU:0, one launch (start us, length us, event | category | flops | bytes accessed | tf_op | source)
XLA Modules:
  0.0 100.4 jit_solution(6810859410955828517)
XLA Ops:
  0.6 0.0 copy-start.11
  0.6 1.2 %fusion.11 = (bf16[186,8,128]{2,1,0:T(8,128)(2,1)S(1)}, bf16[186,8,128]{2,1,0:T(8,128)(2,1)S(1)}) fusion(bf16[186,64,128]{2,1,0:T(8,128)(2,1)} %x_ref.3), kind=kLoop, calls=%fused_computation.38 | loop fusion | bytes 1523712 | tf_op jit(solution)/shard_map/slice | solution.py:219
  1.9 0.0 copy-start.12
  1.9 1.1 %copy.56 = bf16[186,8,128]{0,2,1:T(8,128)(2,1)} copy(bf16[186,8,128]{2,1,0:T(8,128)(2,1)S(1)} %get-tuple-element.22) | data formatting | bytes 761856
  3.0 0.5 collective-permute-start
  3.5 1.1 %copy.57 = bf16[186,8,128]{0,2,1:T(8,128)(2,1)} copy(bf16[186,8,128]{2,1,0:T(8,128)(2,1)S(1)} %get-tuple-element.21) | data formatting | bytes 761856
  4.6 1.9 %collective-permute-start.1 = (bf16[186,8,128]{0,2,1:T(8,128)(2,1)}, bf16[186,8,128]{0,2,1:T(8,128)(2,1)}, u32[]{:S(2)}, u32[]{:S(2)}) collective-permute-start(bf16[186,8,128]{0,2,1:T(8,128)(2,1)} %copy.57), channel_id=1, source_target_pairs={{8,0},{16,8},{24,16},{0,24},{9,1},{17,9},{25,17},{1,25},{10,2},{18... | collective-permute-start | bytes 1142792 | tf_op jit(solution)/shard_map/ppermute | solution.py:219
  6.5 0.0 copy-done.11
  6.5 1.2 %reshape_squeeze.3 = bf16[128,4,512]{2,1,0:T(4,128)(2,1)} reshape(bf16[128,1,1,2048]{3,0,2,1:T(8,128)(2,1)S(1)} %copy-done.11) | data formatting | bytes 1048576 | tf_op jit(solution)/shard_map/reshape;squeeze | solution.py:210
  7.7 1.3 %copy.61 = bf16[128,4,512]{2,0,1:T(8,128)(2,1)S(1)} copy(bf16[128,4,512]{2,1,0:T(4,128)(2,1)} %reshape_squeeze.3) | data formatting | bytes 1048576 | tf_op jit(solution)/shard_map/reshape;squeeze | solution.py:210
  9.0 0.0 copy-done.12
  9.0 1.0 pad_maximum_fusion
  10.0 5.7 %all-to-all-start = ((bf16[4,128,768]{2,1,0:T(8,128)(2,1)}), bf16[4,128,768]{2,1,0:T(8,128)(2,1)}, u32[]{:S(2)}, u32[]{:S(2)}) async-start(bf16[4,128,768]{2,1,0:T(8,128)(2,1)} %pad_maximum_fusion), calls=%async_computation | async-start | bytes 1572864 | tf_op jit(solution)/shard_map/all_to_all | solution.py:214
  15.7 0.0 copy-done
  15.7 0.0 copy-start.15
  15.7 4.1 %fusion.10 = (bf16[186,64,8]{2,1,0:T(8,128)(2,1)}, bf16[186,64,8]{2,1,0:T(8,128)(2,1)}) fusion(bf16[186,64,128]{2,1,0:T(8,128)(2,1)S(1)} %copy-done), kind=kLoop, calls=%fused_computation.37 | loop fusion | bytes 761856 | tf_op jit(solution)/shard_map/slice | solution.py:251
  19.8 0.0 copy-done.13
  19.8 0.8 copy.36
  20.6 1.0 broadcast_multiply_fusion.1.w1_ref
  21.6 0.0 copy-done.18
  21.6 0.9 copy.39.b1_ref
  22.5 0.0 copy-done.15
  22.5 0.9 copy.40.gain_ref
  24.0 2.7 %broadcast_multiply_fusion.e1_ref = bf16[512,1536]{1,0:T(8,128)(2,1)} fusion(bf16[512,1536]{1,0:T(8,128)(2,1)} %param.20), kind=kLoop, calls=%fused_computation.1 | loop fusion | flops 786432 | bytes 3145728 | tf_op jit(solution)/shard_map/mul | solution.py:266
  26.8 0.7 and_select_fusion
  27.5 0.0 copy-start.1
  27.5 0.9 copy-done.1
  28.5 0.9 copy-done.3
  29.4 1.0 %copy-done.5 = bf16[512,512]{1,0:T(8,128)(2,1)S(1)} copy-done((bf16[512,512]{1,0:T(8,128)(2,1)S(1)}, bf16[512,512]{1,0:T(8,128)(2,1)}, u32[]{:S(2)}) %copy-start.5) | copy-done | bytes 524312
  30.5 9.1 %shard_map.158 = (bf16[128,64,128]{2,1,0:T(8,128)(2,1)}, f32[192,512]{1,0:T(8,128)S(1)}) custom-call(s32[1]{0:T(128)} %bitcast.8.place_ref, bf16[186,64,128]{2,1,0:T(8,128)(2,1)S(1)} %copy-done, bf16[512,192]{1,0:T(8,128)(2,1)S(1)} %pad.4.w1_ref, f32[512,1]{1,0:T(8,128)S(1)} %copy-done.1, bf16[512,512]{1,0:T(8,128)(2,1)S(1)} %copy-done.5, ...), custom_call_target="tpu_custom_call" | custom-call | flops 7516192768 | bytes 2572288 | tf_op jit(solution)/shard_map/pallas_call | solution.py:86
  39.5 9.1 %shard_map.159 = (bf16[128,64,128]{2,1,0:T(8,128)(2,1)}, f32[192,512]{1,0:T(8,128)S(1)}) custom-call(s32[1]{0:T(128)} %bitcast.8.place_ref, bf16[186,64,128]{2,1,0:T(8,128)(2,1)S(1)} %copy-done, bf16[512,192]{1,0:T(8,128)(2,1)S(1)} %pad.4.w1_ref, f32[512,1]{1,0:T(8,128)S(1)} %copy-done.1, ...), custom_call_target="tpu_custom_call", output_to_operand_aliasing={{0}: (7, {})} | custom-call | flops 7516192768 | bytes 2572288 | tf_op jit(solution)/shard_map/pallas_call | solution.py:86
  48.6 0.8 copy-done.8
  49.3 0.0 copy-done.14
  49.4 4.4 %copy.58 = bf16[186,64,8]{0,2,1:T(8,128)(2,1)} copy(bf16[186,64,8]{2,1,0:T(8,128)(2,1)} %get-tuple-element.20) | data formatting | bytes 380928
  53.8 0.0 copy-done.10
  53.8 3.2 %copy.59 = bf16[186,64,8]{0,2,1:T(8,128)(2,1)} copy(bf16[186,64,8]{2,1,0:T(8,128)(2,1)S(1)} %copy-done.10) | data formatting | bytes 380928
  57.0 0.0 collective-permute-done
  57.0 0.8 fusion.12
  57.8 0.0 collective-permute-done.1
  57.8 0.8 fusion.13
  58.6 1.0 %maximum_bitcast_fusion = bf16[186,640]{0,1:T(8,128)(2,1)S(1)} fusion(bf16[186,8,8]{0,2,1:T(8,128)(2,1)S(1)} %get-tuple-element.26, bf16[186,64,8]{0,2,1:T(8,128)(2,1)} %copy.58, bf16[186,8,8]{0,2,1:T(8,128)(2,1)S(1)} %get-tuple-element.24), kind=kLoop, calls=%fused_computation.3 | loop fusion | flops 238080 | bytes 476160 | tf_op jit(solution)/shard_map/reshape | solution.py:256
  59.6 0.0 copy-start.6
  59.6 0.9 copy.46
  60.5 1.5 %collective-permute-start.2 = (bf16[186,640]{1,0:T(8,128)(2,1)}, bf16[186,640]{1,0:T(8,128)(2,1)S(1)}, u32[]{:S(2)}, u32[]{:S(2)}) collective-permute-start(bf16[186,640]{1,0:T(8,128)(2,1)} %copy.46), channel_id=1, source_target_pairs={{0,4},{4,0},{1,5},{5,1},{2,6},{6,2},{3,7},{7,3},{8,12},{12,8},{9,1... | collective-permute-start | bytes 714248 | tf_op jit(solution)/shard_map/ppermute | solution.py:256
  62.0 1.0 %maximum_bitcast_fusion.1 = bf16[186,640]{0,1:T(8,128)(2,1)S(1)} fusion(bf16[186,8,8]{0,2,1:T(8,128)(2,1)S(1)} %get-tuple-element.25, bf16[186,64,8]{0,2,1:T(8,128)(2,1)} %copy.59, bf16[186,8,8]{0,2,1:T(8,128)(2,1)S(1)} %get-tuple-element.23), kind=kLoop, calls=%fused_computation.4 | loop fusion | flops 238080 | bytes 476160 | tf_op jit(solution)/shard_map/reshape | solution.py:257
  63.0 0.8 copy.48
  63.9 0.5 collective-permute-start.3
  64.4 0.0 copy-done.19
  64.4 0.1 copy.51.eb1_ref
  64.6 0.1 copy.52.mgain_ref
  64.7 0.1 copy.53.mbias_ref
  64.9 0.1 dynamic-slice_select_fusion
  65.0 1.2 %copy.54.up_ref = bf16[186,1024]{1,0:T(8,128)(2,1)S(1)} copy(bf16[186,1024]{0,1:T(8,128)(2,1)} %bitcast.11) | data formatting | bytes 761856 | tf_op jit(solution)/shard_map/reshape | solution.py:264
  66.2 1.2 %copy.55.down_ref = bf16[186,1024]{1,0:T(8,128)(2,1)S(1)} copy(bf16[186,1024]{0,1:T(8,128)(2,1)} %bitcast.12) | data formatting | bytes 761856 | tf_op jit(solution)/shard_map/reshape | solution.py:264
  67.5 2.1 %collective-permute-done.2.left_ref = bf16[186,640]{1,0:T(8,128)(2,1)S(1)} collective-permute-done((bf16[186,640]{1,0:T(8,128)(2,1)}, bf16[186,640]{1,0:T(8,128)(2,1)S(1)}, u32[]{:S(2)}, u32[]{:S(2)}) %collective-permute-start.2) | collective-permute-done | bytes 238112 | tf_op jit(solution)/shard_map/ppermute | solution.py:256
  69.5 4.0 %collective-permute-done.3.right_ref = bf16[186,640]{1,0:T(8,128)(2,1)} collective-permute-done((bf16[186,640]{1,0:T(8,128)(2,1)}, bf16[186,640]{1,0:T(8,128)(2,1)}, u32[]{:S(2)}, u32[]{:S(2)}) %collective-permute-start.3) | collective-permute-done | bytes 238112 | tf_op jit(solution)/shard_map/ppermute | solution.py:257
  73.5 0.0 all-to-all-done
  73.6 0.0 copy-start.7
  73.6 1.0 %copy-done.7 = bf16[512,512]{1,0:T(8,128)(2,1)S(1)} copy-done((bf16[512,512]{1,0:T(8,128)(2,1)S(1)}, bf16[512,512]{1,0:T(8,128)(2,1)}, u32[]{:S(2)}) %copy-start.7) | copy-done | bytes 524312
  74.6 1.0 copy-done.9
  75.6 6.2 %shard_map.160 = (f32[512,256]{1,0:T(8,128)}, f32[8,256]{1,0:T(8,128)S(1)}) custom-call(bf16[512,768]{1,0:T(8,128)(2,1)} %bitcast.2.moved_ref, s32[1,2048]{1,0:T(1,128)S(1)} %get-tuple-element.17.near_ref, s32[3,512]{1,0:T(4,128)S(1)} %pad_add_fusion.send_ref, f32[192,512]{1,0:T(8,128)S(1)} %copy-done.9, bf16[186,1024]{1,0:T(8,128)(2,1)S(1)} %copy.54.up_ref, ...), custom_call_target="tpu_custom_call" | custom-call | flops 4000000000 | bytes 8000000 | tf_op jit(solution)/shard_map/pallas_call | solution.py:166
  81.8 4.8 %all-to-all-start.1 = ((f32[4,128,256]{2,1,0:T(8,128)}), f32[4,128,256]{2,1,0:T(8,128)S(1)}, u32[]{:S(2)}, u32[]{:S(2)}) async-start(f32[4,128,256]{2,1,0:T(8,128)} %bitcast.18), calls=%async_computation.1 | async-start | bytes 1048576 | tf_op jit(solution)/shard_map/all_to_all | solution.py:271
  86.6 13.1 %all-to-all-done.1 = f32[4,128,256]{2,1,0:T(8,128)S(1)} async-done(((f32[4,128,256]{2,1,0:T(8,128)}), f32[4,128,256]{2,1,0:T(8,128)S(1)}, u32[]{:S(2)}, u32[]{:S(2)}) %all-to-all-start.1) | async-done | bytes 524320 | tf_op jit(solution)/shard_map/all_to_all | solution.py:271
  99.7 0.7 fusion.1
  (28 shorter events, 0.2 us)
Async XLA Ops:
  0.6 5.9 %copy-start.11 = (bf16[128,1,1,2048]{3,0,2,1:T(8,128)(2,1)S(1)}, bf16[128,1,1,2048]{3,0,2,1:T(8,128)(2,1)}, u32[]{:S(2)}) copy-start(bf16[128,1,1,2048]{3,0,2,1:T(8,128)(2,1)} %param.26) | copy-start | bytes 1572868
  1.9 7.1 %copy-start.12 = (bf16[128,1,1,256]{3,0,2,1:T(8,128)(2,1)S(1)}, bf16[128,1,1,256]{3,0,2,1:T(8,128)(2,1)}, u32[]{:S(2)}) copy-start(bf16[128,1,1,256]{3,0,2,1:T(8,128)(2,1)} %param.25) | copy-start | bytes 196612
  3.0 54.0 %collective-permute-start = (bf16[186,8,128]{0,2,1:T(8,128)(2,1)}, bf16[186,8,128]{0,2,1:T(8,128)(2,1)}, u32[]{:S(2)}, u32[]{:S(2)}) collective-permute-start(bf16[186,8,128]{0,2,1:T(8,128)(2,1)} %copy.56), channel_id=1, source_target_pairs={{0,8},{8,16},{16,24},{24,0},{1,9},{9,17},{17,25},{25,1},{2,10},{10... | collective-permute-start | bytes 1142792 | tf_op jit(solution)/shard_map/ppermute | solution.py:218
  4.6 53.2 %collective-permute-start.1 = (bf16[186,8,128]{0,2,1:T(8,128)(2,1)}, bf16[186,8,128]{0,2,1:T(8,128)(2,1)}, u32[]{:S(2)}, u32[]{:S(2)}) collective-permute-start(bf16[186,8,128]{0,2,1:T(8,128)(2,1)} %copy.57), channel_id=1, source_target_pairs={{8,0},{16,8},{24,16},{0,24},{9,1},{17,9},{25,17},{1,25},{10,2},{18... | collective-permute-start | bytes 1142792 | tf_op jit(solution)/shard_map/ppermute | solution.py:219
  7.7 8.0 %copy-start = (bf16[186,64,128]{2,1,0:T(8,128)(2,1)S(1)}, bf16[186,64,128]{2,1,0:T(8,128)(2,1)}, u32[]{:S(2)}) copy-start(bf16[186,64,128]{2,1,0:T(8,128)(2,1)} %x_ref.3) | copy-start | bytes 9142276
  10.0 63.6 %all-to-all-start = ((bf16[4,128,768]{2,1,0:T(8,128)(2,1)}), bf16[4,128,768]{2,1,0:T(8,128)(2,1)}, u32[]{:S(2)}, u32[]{:S(2)}) async-start(bf16[4,128,768]{2,1,0:T(8,128)(2,1)} %pad_maximum_fusion), calls=%async_computation | async-start | bytes 1572864 | tf_op jit(solution)/shard_map/all_to_all | solution.py:214
  15.7 4.1 %copy-start.13 = (bf16[512,186]{0,1:T(8,128)(2,1)S(1)}, bf16[512,186]{0,1:T(8,128)(2,1)}, u32[]{:S(2)}) copy-start(bf16[512,186]{0,1:T(8,128)(2,1)} %param.16) | copy-start | bytes 571396
  15.7 6.0 %copy-start.18 = (f32[512]{0:T(512)S(1)}, f32[512]{0:T(512)}, u32[]{:S(2)}) copy-start(f32[512]{0:T(512)} %param.17) | copy-start | bytes 6148
  15.7 6.8 %copy-start.15 = (f32[512]{0:T(512)S(1)}, f32[512]{0:T(512)}, u32[]{:S(2)}) copy-start(f32[512]{0:T(512)} %param.19) | copy-start | bytes 6148
  27.5 1.0 copy-start.1
  28.5 0.9 copy-start.3
  29.4 1.0 %copy-start.5 = (bf16[512,512]{1,0:T(8,128)(2,1)S(1)}, bf16[512,512]{1,0:T(8,128)(2,1)}, u32[]{:S(2)}) copy-start(bf16[512,512]{1,0:T(8,128)(2,1)} %w2_ref.5) | copy-start | bytes 1572868
  39.5 9.8 %copy-start.14 = (s32[1,1,2048]{2,1,0:T(1,128)S(1)}, s32[1,1,2048]{2,1,0:T(1,128)}, u32[]{:S(2)}) copy-start(s32[1,1,2048]{2,1,0:T(1,128)} %param.28) | copy-start | bytes 24580
  48.6 0.8 copy-start.8
  49.3 4.5 %copy-start.10 = (bf16[186,64,8]{2,1,0:T(8,128)(2,1)S(1)}, bf16[186,64,8]{2,1,0:T(8,128)(2,1)}, u32[]{:S(2)}) copy-start(bf16[186,64,8]{2,1,0:T(8,128)(2,1)} %get-tuple-element.19) | copy-start | bytes 571396
  57.0 7.4 %copy-start.19 = (f32[512]{0:T(512)S(1)}, f32[512]{0:T(512)}, u32[]{:S(2)}) copy-start(f32[512]{0:T(512)} %param.21) | copy-start | bytes 6148
  57.0 7.6 %copy-start.16 = (f32[512]{0:T(512)S(1)}, f32[512]{0:T(512)}, u32[]{:S(2)}) copy-start(f32[512]{0:T(512)} %param.23) | copy-start | bytes 6148
  57.0 7.7 %copy-start.17 = (f32[512]{0:T(512)S(1)}, f32[512]{0:T(512)}, u32[]{:S(2)}) copy-start(f32[512]{0:T(512)} %param.24) | copy-start | bytes 6148
  59.6 13.9 %copy-start.2 = (f32[512,1]{1,0:T(8,128)S(1)}, f32[512,1]{1,0:T(8,128)}, u32[]{:S(2)}) copy-start(f32[512,1]{1,0:T(8,128)} %copy.39.b1_ref) | copy-start | bytes 6148
  59.6 13.9 %copy-start.4 = (f32[512,1]{1,0:T(8,128)S(1)}, f32[512,1]{1,0:T(8,128)}, u32[]{:S(2)}) copy-start(f32[512,1]{1,0:T(8,128)} %copy.40.gain_ref) | copy-start | bytes 6148
  59.6 13.9 %copy-start.6 = (bf16[512,512]{1,0:T(8,128)(2,1)S(1)}, bf16[512,512]{1,0:T(8,128)(2,1)}, u32[]{:S(2)}) copy-start(bf16[512,512]{1,0:T(8,128)(2,1)} %w2_ref.5) | copy-start | bytes 1572868
  60.5 9.0 %collective-permute-start.2 = (bf16[186,640]{1,0:T(8,128)(2,1)}, bf16[186,640]{1,0:T(8,128)(2,1)S(1)}, u32[]{:S(2)}, u32[]{:S(2)}) collective-permute-start(bf16[186,640]{1,0:T(8,128)(2,1)} %copy.46), channel_id=1, source_target_pairs={{0,4},{4,0},{1,5},{5,1},{2,6},{6,2},{3,7},{7,3},{8,12},{12,8},{9,1... | collective-permute-start | bytes 714248 | tf_op jit(solution)/shard_map/ppermute | solution.py:256
  63.9 9.6 %collective-permute-start.3 = (bf16[186,640]{1,0:T(8,128)(2,1)}, bf16[186,640]{1,0:T(8,128)(2,1)}, u32[]{:S(2)}, u32[]{:S(2)}) collective-permute-start(bf16[186,640]{1,0:T(8,128)(2,1)} %copy.48), channel_id=1, source_target_pairs={{4,0},{0,4},{5,1},{1,5},{6,2},{2,6},{7,3},{3,7},{12,8},{8,12},{13,... | collective-permute-start | bytes 714248 | tf_op jit(solution)/shard_map/ppermute | solution.py:257
  73.6 1.0 %copy-start.7 = (bf16[512,512]{1,0:T(8,128)(2,1)S(1)}, bf16[512,512]{1,0:T(8,128)(2,1)}, u32[]{:S(2)}) copy-start(bf16[512,512]{1,0:T(8,128)(2,1)} %e2_ref.1) | copy-start | bytes 1572868
  74.6 1.0 copy-start.9
  81.8 17.9 %all-to-all-start.1 = ((f32[4,128,256]{2,1,0:T(8,128)}), f32[4,128,256]{2,1,0:T(8,128)S(1)}, u32[]{:S(2)}, u32[]{:S(2)}) async-start(f32[4,128,256]{2,1,0:T(8,128)} %bitcast.18), calls=%async_computation.1 | async-start | bytes 1048576 | tf_op jit(solution)/shard_map/all_to_all | solution.py:271

commit v2 on v0

v2 whole, which is shorter than its diff:
```python
import jax
import jax.numpy as jnp
from jax import lax
from jax.experimental import pallas as pl
from jax.experimental.pallas import tpu as pltpu
from jax.sharding import PartitionSpec as P

HALO = 8
ROWS = 16
GROUP = 4

epsilon = 1e-05
F32 = jnp.float32
BF16 = jnp.bfloat16


def half_silu(half):
    return half + half * jnp.tanh(half)


def centre(values):
    average = jnp.mean(values, axis=0, keepdims=True)
    centred = values - average
    spread = jnp.mean(centred * centred, axis=0, keepdims=True)
    return average, lax.rsqrt(spread + epsilon)


def onehot_of(index_row, first, count):
    ids = lax.broadcasted_iota(jnp.int32, (count, index_row.shape[1]), 0)
    return jnp.where(ids == index_row - first, 1.0, 0.0).astype(BF16)


MESH = pl.DeviceIdType.MESH


def partner(dx, dy, dz):
    ids = {}
    for axis, step in (("gx", dx), ("gy", dy), ("gz", dz)):
        size = lax.axis_size(axis)
        ids[axis] = lax.rem(lax.axis_index(axis) + (step + size), size)
    return ids


def kernel(
    x_hbm, w1_ref, w2_ref, e1_ref, e2_ref, vec_ref, mesh_ref, edge_ref, near_ref, send_ref,
    out_hbm, mesh_out_ref,
    x_ref, wide, w1, cols, gathered, pre_ref, out_wide, stage,
    rows_send, cols_send, rows_recv, cols_recv, corner_recv,
    assigned, nodes_all, totals, parts,
    x_sem, out_sem, halo_send, halo_recv, z_send, z_recv,
):
    tiles, channels, rows, lon = x_ref.shape
    padded = w1.shape[1]
    latent, share = assigned.shape
    shard, nodes = mesh_ref.shape
    slots = edge_ref.shape[1]
    layers = slots // share
    me = lax.axis_index("gz")
    mine = pl.ds(pl.multiple_of(me * shard, shard), shard)

    diagonals = ((1, 1), (1, -1), (-1, 1), (-1, -1))
    around = [(1, 0, 0), (-1, 0, 0), (0, 1, 0), (0, -1, 0)]
    around += [(dx, dy, 0) for dx, dy in diagonals]
    around += [(0, 0, k) for k in range(1, layers)]
    barrier = pltpu.get_barrier_semaphore()
    for offset in around:
        pl.semaphore_signal(barrier, inc=1, device_id=partner(*offset), device_id_type=MESH)
    loads = [
        pltpu.make_async_copy(x_hbm.at[:, pl.ds(t * rows, rows), :], x_ref.at[t], x_sem.at[t])
        for t in range(tiles)
    ]
    for load in loads:
        load.start()

    w1[...] = jnp.zeros_like(w1)
    w1[:, :channels] = w1_ref[...] * 0.5
    cols[...] = vec_ref[...].T
    b1, gain = cols[:, 0:1] * 0.5, cols[:, 1:2]
    gathered[...] = jnp.zeros_like(gathered)
    assigned[mine, :] = edge_ref[:, pl.ds(pl.multiple_of(me * share, share), share)]
    nodes_all[mine, :] = mesh_ref[...]
    pl.semaphore_wait(barrier, len(around))

    def remote(source, target, send_sem, recv_sem, offset):
        return pltpu.make_async_remote_copy(
            src_ref=source, dst_ref=target, send_sem=send_sem, recv_sem=recv_sem,
            device_id=partner(*offset), device_id_type=MESH,
        )

    spread = []
    for k in range(1, layers):
        peer = lax.rem(me + k, layers)
        theirs = pl.ds(pl.multiple_of(peer * share, share), share)
        spread.append(
            remote(edge_ref.at[:, theirs], assigned.at[mine, :], z_send.at[0, k], z_recv.at[0, k], (0, 0, k))
        )
        spread.append(
            remote(mesh_ref, nodes_all.at[mine, :], z_send.at[1, k], z_recv.at[1, k], (0, 0, k))
        )
    for copy in spread:
        copy.start()

    def widen(t, carry):
        wide[t, pl.ds(0, channels * rows), :] = x_ref[t].astype(F32).reshape(channels * rows, lon)
        wide[t, pl.ds(channels * rows, (padded - channels) * rows), :] = jnp.zeros(
            ((padded - channels) * rows, lon), F32
        )
        lanes = lax.broadcasted_iota(jnp.int32, (padded, lon), 1) // HALO
        left = jnp.zeros((padded, lon), F32)
        right = jnp.zeros((padded, lon), F32)
        for j in range(rows):
            row = wide[t, pl.ds(j, padded, stride=rows), :]
            here = lanes == j
            left = jnp.where(here, row if j == 0 else pltpu.roll(row, j * HALO, 1), left)
            turn = (j * HALO + HALO) % lon
            right = jnp.where(here, row if turn == 0 else pltpu.roll(row, turn, 1), right)
        cols_send[0, t] = left.astype(BF16)
        cols_send[1, t] = right.astype(BF16)
        return carry

    for load in loads:
        load.wait()
    lax.fori_loop(0, tiles, widen, 0)
    for j in range(HALO):
        at = pl.ds(j * lon, lon)
        rows_send[0, :, at] = wide[0, pl.ds(j, padded, stride=rows), :].astype(BF16)
        rows_send[1, :, at] = wide[
            tiles - 1, pl.ds(rows - HALO + j, padded, stride=rows), :
        ].astype(BF16)

    def embed(t):
        slot = 0
        own_gain = cols[mine, 1:2]
        for group in range(rows // GROUP):
            cells = jnp.concatenate(
                [wide[t, pl.ds(group * GROUP + r, padded, stride=rows), :] for r in range(GROUP)],
                axis=1,
            ).astype(BF16)
            half = jnp.dot(w1[...], cells, preferred_element_type=F32) + b1
            hidden = half_silu(half).astype(BF16)
            slot = group % 2
            pre_ref[slot] = jnp.dot(w2_ref[...], hidden, preferred_element_type=F32)
            average, scale = centre(pre_ref[slot])
            own = (pre_ref[slot, mine, :] - average) * scale * own_gain
            for r in range(GROUP):
                out_wide[pl.ds(group * GROUP + r, shard, stride=rows), :] = own[
                    :, r * lon : (r + 1) * lon
                ]
            first = (t * rows + group * GROUP) * lon
            pick = onehot_of(send_ref[0:1, :], first, GROUP * lon)
            gathered[...] += jnp.dot(cells, pick, preferred_element_type=F32)
        stage[t] = out_wide[...].reshape(shard, rows, lon).astype(BF16)

    def store(t):
        return pltpu.make_async_copy(
            stage.at[t], out_hbm.at[:, pl.ds(t * rows, rows), :], out_sem.at[t]
        )

    halo = [
        remote(rows_send.at[1], rows_recv.at[0], halo_send.at[0], halo_recv.at[0], (1, 0, 0)),
        remote(rows_send.at[0], rows_recv.at[1], halo_send.at[1], halo_recv.at[1], (-1, 0, 0)),
        remote(cols_send.at[1], cols_recv.at[0], halo_send.at[2], halo_recv.at[2], (0, 1, 0)),
        remote(cols_send.at[0], cols_recv.at[1], halo_send.at[3], halo_recv.at[3], (0, -1, 0)),
    ]
    for i, (dx, dy) in enumerate(diagonals):
        halo.append(
            remote(
                cols_send.at[1 if dy > 0 else 0, tiles - 1 if dx > 0 else 0],
                corner_recv.at[i], halo_send.at[4 + i], halo_recv.at[4 + i], (dx, dy, 0),
            )
        )
    for copy in halo:
        copy.start()

    def advance(t, carry):
        embed(t)
        store(t).start()
        return carry

    lax.fori_loop(0, tiles, advance, 0)

    for copy in halo:
        copy.wait()
    picked = gathered[...]
    first = 0
    pieces = [rows_recv[0], rows_recv[1]]
    pieces += [cols_recv[side, t] for side in range(2) for t in range(tiles)]
    pieces += [corner_recv[i] for i in range(4)]
    for piece in pieces:
        pick = onehot_of(send_ref[1:2, :], first, piece.shape[1])
        picked = picked + jnp.dot(piece, pick, preferred_element_type=F32)
        first += piece.shape[1]
    half = jnp.dot(w1[...], picked.astype(BF16), preferred_element_type=F32) + b1
    pre = jnp.dot(w2_ref[...], half_silu(half).astype(BF16), preferred_element_type=F32)
    average, scale = centre(pre)
    sender = ((pre - average) * scale * gain).astype(BF16)
    for copy in spread:
        copy.wait()
    onehot = onehot_of(send_ref[2:3, :], 0, nodes)
    mesh_cols = jnp.dot(nodes_all[...], onehot, preferred_element_type=F32).astype(BF16)
    half = jnp.dot(e1_ref[:, :latent], assigned[...], preferred_element_type=F32)
    half = half + jnp.dot(e1_ref[:, latent : 2 * latent], sender, preferred_element_type=F32)
    half = half + jnp.dot(e1_ref[:, 2 * latent :], mesh_cols, preferred_element_type=F32)
    hidden = half_silu((half + cols[:, 2:3]) * 0.5).astype(BF16)
    second = jnp.dot(e2_ref[...], hidden, preferred_element_type=F32)
    average, scale = centre(second)
    message = (
        assigned[...].astype(F32) + (second - average) * scale * cols[:, 3:4] + cols[:, 4:5]
    ).astype(BF16)
    last = (((1,), (1,)), ((), ()))
    totals[...] = lax.dot_general(message, onehot, last, preferred_element_type=F32)
    parts[0] = totals[mine, :]
    exchange = []
    for k in range(1, layers):
        peer = lax.rem(me + k, layers)
        theirs = pl.ds(pl.multiple_of(peer * shard, shard), shard)
        exchange.append(
            remote(totals.at[theirs, :], parts.at[k], z_send.at[2, k], z_recv.at[2, k], (0, 0, k))
        )
    for copy in exchange:
        copy.start()
    degree = jnp.zeros((8, nodes), F32)
    for start in range(0, slots, share):
        chunk = onehot_of(near_ref[:, start : start + share], 0, nodes)
        ones = jnp.ones((8, share), BF16)
        degree = degree + lax.dot_general(ones, chunk, last, preferred_element_type=F32)
    scale = jnp.maximum(degree[:1], 1.0)
    for copy in exchange:
        copy.wait()
    total = parts[0]
    for k in range(1, layers):
        total = total + parts[k]
    mesh_out_ref[...] = (mesh_ref[...].astype(F32) + total / scale).astype(BF16)
    for t in range(tiles):
        store(t).wait()


def on_device(
    grid_inputs,
    embed_w1,
    embed_b1,
    embed_w2,
    embed_gain,
    edge_w1,
    edge_b1,
    edge_w2,
    message_gain,
    message_bias,
    mesh_latent,
    edge_latent,
    senders,
    receivers,
    edge_counts,
):
    latent = embed_w2.shape[0]
    channels, lat, lon = grid_inputs.shape
    shard = mesh_latent.shape[0]
    nodes = mesh_latent.shape[3]
    slots = edge_latent.shape[3]
    layers = lax.axis_size("gz")
    layer = lax.axis_index("gz")
    band = lax.axis_index("gx")
    sector = lax.axis_index("gy")
    lon_total = lon * lax.axis_size("gy")
    share = slots // layers
    padded = -(-channels // 16) * 16
    tiles = lat // ROWS

    slot_ids = jnp.arange(slots, dtype=jnp.int32)
    tile = band * lax.axis_size("gy") + sector
    near = jnp.where(slot_ids < edge_counts[0, 0], receivers[0, 0] - tile * nodes, -1)
    my_near = lax.dynamic_slice_in_dim(near, layer * share, share)
    send = lax.dynamic_slice_in_dim(senders[0, 0], layer * share, share)
    row = send // lon_total - band * lat
    column = (send % lon_total - sector * lon + HALO + lon_total) % lon_total - HALO
    above, below = row < 0, row >= lat
    west, east = column < 0, column >= lon
    inside_row = ~(above | below)
    inside_column = ~(west | east)
    own_index = jnp.where(inside_row & inside_column, row * lon + column, -1)
    strip = HALO * lon
    tall = lat * HALO
    row_index = jnp.where(above, row + HALO, row - lat + HALO) * lon + column
    beside = jnp.where(west, column + HALO, column - lon)
    column_index = 2 * strip + jnp.where(west, 0, tall) + row * HALO + beside
    corner = jnp.where(above, 0, 2) + jnp.where(west, 0, 1)
    corner_row = jnp.where(above, row + ROWS, row - lat)
    corner_index = 2 * (strip + tall) + (corner * ROWS + corner_row) * HALO + beside
    halo_index = jnp.where(
        inside_column,
        jnp.where(inside_row, -1, row_index),
        jnp.where(inside_row, column_index, corner_index),
    )
    send_table = jnp.stack([own_index, halo_index, my_near])
    empty = jnp.zeros_like(embed_b1)
    vectors = jnp.stack(
        [embed_b1, embed_gain, edge_b1, message_gain, message_bias, empty, empty, empty]
    )

    vmem = pl.BlockSpec(memory_space=pltpu.VMEM)
    hbm = pl.BlockSpec(memory_space=pl.ANY)
    scratch = [
        ((tiles, channels, ROWS, lon), BF16),
        ((tiles, padded * ROWS, lon), F32),
        ((latent, padded), BF16),
        ((latent, 8), F32),
        ((padded, share), F32),
        ((2, latent, GROUP * lon), F32),
        ((shard * ROWS, lon), F32),
        ((tiles, shard, ROWS, lon), BF16),
        ((2, padded, strip), BF16),
        ((2, tiles, padded, lon), BF16),
        ((2, padded, strip), BF16),
        ((2, tiles, padded, lon), BF16),
        ((4, padded, lon), BF16),
        ((latent, share), BF16),
        ((latent, nodes), BF16),
        ((latent, nodes), F32),
        ((layers, shard, nodes), F32),
    ]
    sems = [(tiles,), (tiles,), (8,), (8,), (3, layers), (3, layers)]
    grid_out, mesh_out = pl.pallas_call(
        kernel,
        in_specs=[hbm] + [vmem] * 9,
        out_specs=[hbm, vmem],
        out_shape=[
            jax.ShapeDtypeStruct((shard, lat, lon), BF16),
            jax.ShapeDtypeStruct((shard, nodes), BF16),
        ],
        scratch_shapes=[pltpu.VMEM(s, d) for s, d in scratch]
        + [pltpu.SemaphoreType.DMA(s) for s in sems],
        compiler_params=pltpu.CompilerParams(
            collective_id=0, has_side_effects=True, vmem_limit_bytes=60 * 1024 * 1024
        ),
    )(
        grid_inputs, embed_w1, embed_w2, edge_w1, edge_w2, vectors,
        mesh_latent[:, 0, 0, :], edge_latent[:, 0, 0, :], near[None], send_table,
    )
    return (mesh_out.reshape(shard, 1, 1, nodes), grid_out)


def solution(mesh):
    return jax.shard_map(
        on_device,
        mesh=mesh,
        in_specs=(
            P(None, "gx", "gy"),
            P(),
            P(),
            P(),
            P(),
            P(),
            P(),
            P(),
            P(),
            P(),
            P("gz", "gx", "gy", None),
            P("gz", "gx", "gy", None),
            P("gx", "gy", None),
            P("gx", "gy", None),
            P("gx", "gy"),
        ),
        out_specs=(P("gz", "gx", "gy", None), P("gz", "gx", "gy")),
        check_vma=False,
    )
```

time: 167 us -> 56.8 us (0.34)
  Pallas kernels: 0 us -> 44.2 us
  waiting for transfers between devices: 40.2 us -> 0 us
  other arithmetic: 31 us -> 2.73 us
  local copies, waits for them, and re-layouts: 34.7 us -> 7.7 us
  matrix products: 21.9 us -> 0 us
  blocking collectives: 14 us -> 0 us
  between operations: 15 us -> 1.32 us
  starting transfers between devices: 10.1 us -> 0 us
    pallas_call x0 -> x1, Pallas kernels: none -> 44.2 us  [on_device(): pl.pallas_call(kernel, in_specs=[hbm] + [vmem] * 9, out_specs=[hbm, vmem]...]
    ppermute x4 -> x0, waiting for transfers between devices: 22.7 us -> none  [the longest x2 12.3 us: padded_2(): after = lax.ppermute(first, axis, down)]
    dot_general x6 -> x0, matrix products: 21.9 us -> none  [the longest x1 14.6 us: embed_cells(): jnp.dot(embed_w2, grid_hidden, preferred_element_type=jnp.float32)]
    reduce_scatter x1 -> x0, waiting for transfers between devices: 17.5 us -> none  [on_device(): lax.psum_scatter(partial_totals, 'gz', scatter_dimension=0, tiled=True)]
    gather x3 -> x0, local copies, waits for them, and re-layouts: 14.2 us -> none  [the longest x1 7.91 us: advance_full(): grid_cols = jnp.take(pad_flat, my_grid, axis=1)]
    all_gather x1 -> x0, blocking collectives: 14 us -> none  [on_device(): mesh_full = lax.all_gather(mesh_own, 'gz', axis=0, tiled=True)]
    concatenate x1 -> x0, other arithmetic: 12.1 us -> none  [padded_2(): value = jnp.concatenate([before, value, after], axis=dim)]
    reduce_sum x3 -> x0, other arithmetic: 10.2 us -> none  [the longest x2 8.8 us: normalize(): spread = jnp.mean(centred * centred, axis=0, keepdims=True)]
  transfers between devices with their start and end apart: 6 -> 0, of which waited for: 4 -> 0; matrix products, arithmetic and copies ran while one was open for 11% -> 0% of each run, Pallas kernels for 0% -> 0%
where the time goes in v2:
time: 56.8 us; the launch traced here: 55.9 us
  Pallas kernels  44.2 us (78%)
  local copies, waits for them, and re-layouts  7.7 us (14%)
  other arithmetic  2.73 us (5%)
  between operations  1.32 us (2%)
    pallas_call x1, Pallas kernels, on_device(): pl.pallas_call(kernel, in_specs=[hbm] + [vmem] * 9, out_specs=[hbm, vmem]...  44.2 us
    unnamed x3, local copies, waits for them, and re-layouts  6.32 us
    another operation x3, local copies, waits for them, and re-layouts, on_device(): jnp.stack([embed_b1, embed_gain, edge_b1, message_gain, message_bias, emp...  1.38 us
    select_n x2, other arithmetic, on_device(): jnp.where(slot_ids < edge_counts[0, 0], receivers[0, 0] - tile * nodes, -1)  1.37 us

profile of v2, /device:TPU:0, one launch (start us, length us, event | category | flops | bytes accessed | tf_op | source)
XLA Modules:
  0.0 55.9 jit_solution(10413553691771118884)
XLA Ops:
  1.3 0.7 %and_select_fusion = (s32[1,512]{1,0:T(1,128)S(1)}, s32[1,512]{1,0:T(1,128)S(1)}, s32[1,512]{1,0:T(1,128)S(1)}) fusion(s32[]{:T(128)S(6)} %mul.70, s32[]{:T(128)S(6)} %mul.69, s32[1,1,2048]{2,1,0:T(1,128)} %param.27, s32[]{:T(128)S(6)} %select_n.170), kind=kLoop, calls=%fused_computation.4 | loop fusion | flops 23552 | bytes 8204 | tf_op jit(solution)/shard_map/jit(_where)/select_n | solution.py:280
  2.1 1.4 %stack.35.vec_ref = f32[8,512]{1,0:T(8,128)} concatenate(f32[1,512]{1,0:T(1,128)} %bitcast.34, f32[1,512]{1,0:T(1,128)} %bitcast.35, f32[1,512]{1,0:T(1,128)} %bitcast.36, f32[1,512]{1,0:T(1,128)} %bitcast.37, f32[1,512]{1,0:T(1,128)} %bitcast.38, f32[1,512]{1,0:T(1,128)S(1)} %stack_broadcast_in_dim.3, f32[2,512]{1,0:T(2,128)S(1)} %stack.34), dimensions={0} | concatenate | bytes 32768 | tf_op jit(solution)/shard_map/stack | solution.py:296
  3.4 1.3 %compare_select_fusion = (s32[1,2048]{1,0:T(1,128)}, s32[1,1,2048]{2,1,0:T(1,128)S(1)}) fusion(s32[]{:T(128)} %bitcast.27, s32[1,1,2048]{2,1,0:T(1,128)} %param.28, s32[]{:T(128)S(6)} %mul.67), kind=kLoop, calls=%fused_computation | loop fusion | flops 6144 | bytes 24584 | tf_op jit(solution)/shard_map/jit(_where)/select_n | solution.py:271
  4.7 0.1 dynamic-slice_select_fusion
  4.8 0.6 %pad_add_fusion.send_ref = s32[3,512]{1,0:T(4,128)} fusion(s32[1,512]{1,0:T(1,128)S(1)} %bitcast.33, s32[1,512]{1,0:T(1,128)S(1)} %select_select_fusion, s32[1,512]{1,0:T(1,128)S(1)} %get-tuple-element.6), kind=kLoop, calls=%fused_computation.3 | loop fusion | flops 3072 | bytes 12288 | tf_op jit(solution)/shard_map/stack | solution.py:294
  5.4 1.8 %copy.17.w1_ref = bf16[512,186]{1,0:T(8,128)(2,1)} copy(bf16[512,186]{0,1:T(8,128)(2,1)} %param.16) | data formatting | bytes 380928 | tf_op args[1]
  7.2 44.2 %shard_map.158 = (bf16[128,64,128]{2,1,0:T(8,128)(2,1)}, bf16[128,256]{1,0:T(8,128)(2,1)}) custom-call(bf16[186,64,128]{2,1,0:T(8,128)(2,1)} %x_hbm.1, bf16[512,186]{1,0:T(8,128)(2,1)} %copy.17.w1_ref, bf16[512,512]{1,0:T(8,128)(2,1)} %w2_ref.1, bf16[512,1536]{1,0:T(8,128)(2,1)} %e1_ref.1, bf16[512,512]{1,0:T(8,128)(2,1)} %e2_ref.1, ...), custom_call_target="tpu_custom_call" | custom-call | tf_op jit(solution)/shard_map/pallas_call | solution.py:322
  51.4 1.5 %copy.21 = bf16[128,1,1,256]{3,0,2,1:T(8,128)(2,1)} copy(bf16[128,1,1,256]{3,0,2,1:T(8,128)(2,1)} %bitcast.31) | data formatting | bytes 131072
  52.8 3.1 %copy.22 = bf16[128,64,128]{2,1,0:T(8,128)(2,1)} copy(bf16[128,64,128]{2,1,0:T(8,128)(2,1)} %get-tuple-element.14) | data formatting | bytes 4194304
  (3 shorter events, 0.0 us)

commit v3 on v2

--- a/solution.py
+++ b/solution.py
@@ -41,13 +41,50 @@
     return ids
 
 
+def split(values, size):
+    if size & (size - 1) == 0:
+        return lax.shift_right_logical(values, size.bit_length() - 1), values & (size - 1)
+    return values // size, values % size
+
+
+def locate(send, receive, live, near_ref, send_ref, nodes, lat, lon):
+    band = lax.axis_index("gx")
+    sector = lax.axis_index("gy")
+    lon_total = lon * lax.axis_size("gy")
+    slot_ids = lax.broadcasted_iota(jnp.int32, receive.shape, 1)
+    tile = band * lax.axis_size("gy") + sector
+    near_ref[...] = jnp.where(slot_ids < live, receive - tile * nodes, -1)
+    row, column = split(send, lon_total)
+    row = row - band * lat
+    column = split(column - sector * lon + (HALO + lon_total), lon_total)[1] - HALO
+    above, below = row < 0, row >= lat
+    west, east = column < 0, column >= lon
+    outside_row = jnp.where(above, 1, jnp.where(below, 1, 0))
+    outside_column = jnp.where(west, 1, jnp.where(east, 1, 0))
+    send_ref[0:1, :] = jnp.where(outside_row + outside_column == 0, row * lon + column, -1)
+    strip = HALO * lon
+    tall = lat * HALO
+    row_index = jnp.where(above, row + HALO, row - lat + HALO) * lon + column
+    beside = jnp.where(west, column + HALO, column - lon)
+    column_index = 2 * strip + jnp.where(west, 0, tall) + row * HALO + beside
+    corner = jnp.where(above, 0, 2) + jnp.where(west, 0, 1)
+    corner_row = jnp.where(above, row + ROWS, row - lat)
+    corner_index = 2 * (strip + tall) + (corner * ROWS + corner_row) * HALO + beside
+    send_ref[1:2, :] = jnp.where(
+        outside_column == 0,
+        jnp.where(outside_row == 0, -1, row_index),
+        jnp.where(outside_row == 0, column_index, corner_index),
+    )
+
+
 def kernel(
-    x_hbm, w1_ref, w2_ref, e1_ref, e2_ref, vec_ref, mesh_ref, edge_ref, near_ref, send_ref,
-    out_hbm, mesh_out_ref,
-    x_ref, wide, w1, cols, gathered, pre_ref, out_wide, stage,
+    x_hbm, w1_ref, w2_ref, e1_hbm, e2_hbm, b1_ref, gain_ref, eb1_ref, mgain_ref, mbias_ref,
+    mesh_ref, edge_ref, senders_ref, receivers_ref, count_ref,
+    out_hbm, mean_ref,
+    x_ref, wide, w1, cols, e1_ref, e2_ref, w1_wide, vec_ref, near_ref, send_ref, gathered, pre_ref, out_wide, stage,
     rows_send, cols_send, rows_recv, cols_recv, corner_recv,
     assigned, nodes_all, totals, parts,
-    x_sem, out_sem, halo_send, halo_recv, z_send, z_recv,
+    x_sem, out_sem, w_sem, halo_send, halo_recv, z_send, z_recv,
 ):
     tiles, channels, rows, lon = x_ref.shape
     padded = w1.shape[1]
@@ -69,12 +106,25 @@
         pltpu.make_async_copy(x_hbm.at[:, pl.ds(t * rows, rows), :], x_ref.at[t], x_sem.at[t])
         for t in range(tiles)
     ]
-    for load in loads:
+    weights = [
+        pltpu.make_async_copy(e1_hbm, e1_ref, w_sem.at[0]),
+        pltpu.make_async_copy(e2_hbm, e2_ref, w_sem.at[1]),
+    ]
+    for load in loads + weights:
         load.start()
 
-    w1[...] = jnp.zeros_like(w1)
-    w1[:, :channels] = w1_ref[...] * 0.5
+    w1_wide[...] = jnp.zeros_like(w1_wide)
+    w1_wide[:channels, :] = w1_ref[...].astype(F32) * 0.5
+    w1[...] = w1_wide[...].T[:, :padded].astype(BF16)
+    vec_ref[...] = jnp.zeros_like(vec_ref)
+    for i, ref in enumerate((b1_ref, gain_ref, eb1_ref, mgain_ref, mbias_ref)):
+        vec_ref[i : i + 1, :] = ref[...]
     cols[...] = vec_ref[...].T
+    locate(
+        senders_ref[:, pl.ds(pl.multiple_of(me * share, share), share)],
+        receivers_ref[...], count_ref[0, 0], near_ref, send_ref, nodes, tiles * rows, lon,
+    )
+    send_ref[2:3, :] = near_ref[:, pl.ds(pl.multiple_of(me * share, share), share)]
     b1, gain = cols[:, 0:1] * 0.5, cols[:, 1:2]
     gathered[...] = jnp.zeros_like(gathered)
     assigned[mine, :] = edge_ref[:, pl.ds(pl.multiple_of(me * share, share), share)]
@@ -101,6 +151,9 @@
         copy.start()
 
     def widen(t, carry):
+        pltpu.make_async_copy(
+            x_hbm.at[:, pl.ds(t * rows, rows), :], x_ref.at[t], x_sem.at[t]
+        ).wait()
         wide[t, pl.ds(0, channels * rows), :] = x_ref[t].astype(F32).reshape(channels * rows, lon)
         wide[t, pl.ds(channels * rows, (padded - channels) * rows), :] = jnp.zeros(
             ((padded - channels) * rows, lon), F32
@@ -118,8 +171,6 @@
         cols_send[1, t] = right.astype(BF16)
         return carry
 
-    for load in loads:
-        load.wait()
     lax.fori_loop(0, tiles, widen, 0)
     for j in range(HALO):
         at = pl.ds(j * lon, lon)
@@ -128,27 +179,30 @@
             tiles - 1, pl.ds(rows - HALO + j, padded, stride=rows), :
         ].astype(BF16)
 
+    def first_layer(t, group):
+        cells = jnp.concatenate(
+            [wide[t, pl.ds(group * GROUP + r, padded, stride=rows), :] for r in range(GROUP)],
+            axis=1,
+        ).astype(BF16)
+        half = jnp.dot(w1[...], cells, preferred_element_type=F32) + b1
+        return cells, half_silu(half).astype(BF16)
+
     def embed(t):
-        slot = 0
         own_gain = cols[mine, 1:2]
+        cells, hidden = first_layer(t, 0)
         for group in range(rows // GROUP):
-            cells = jnp.concatenate(
-                [wide[t, pl.ds(group * GROUP + r, padded, stride=rows), :] for r in range(GROUP)],
-                axis=1,
-            ).astype(BF16)
-            half = jnp.dot(w1[...], cells, preferred_element_type=F32) + b1
-            hidden = half_silu(half).astype(BF16)
             slot = group % 2
             pre_ref[slot] = jnp.dot(w2_ref[...], hidden, preferred_element_type=F32)
+            pick = onehot_of(send_ref[0:1, :], (t * rows + group * GROUP) * lon, GROUP * lon)
+            gathered[...] += jnp.dot(cells, pick, preferred_element_type=F32)
+            if (group + 1) * GROUP < rows:
+                cells, hidden = first_layer(t, group + 1)
             average, scale = centre(pre_ref[slot])
             own = (pre_ref[slot, mine, :] - average) * scale * own_gain
             for r in range(GROUP):
                 out_wide[pl.ds(group * GROUP + r, shard, stride=rows), :] = own[
                     :, r * lon : (r + 1) * lon
                 ]
-            first = (t * rows + group * GROUP) * lon
-            pick = onehot_of(send_ref[0:1, :], first, GROUP * lon)
-            gathered[...] += jnp.dot(cells, pick, preferred_element_type=F32)
         stage[t] = out_wide[...].reshape(shard, rows, lon).astype(BF16)
 
     def store(t):
@@ -198,6 +252,8 @@
         copy.wait()
     onehot = onehot_of(send_ref[2:3, :], 0, nodes)
     mesh_cols = jnp.dot(nodes_all[...], onehot, preferred_element_type=F32).astype(BF16)
+    for copy in weights:
+        copy.wait()
     half = jnp.dot(e1_ref[:, :latent], assigned[...], preferred_element_type=F32)
     half = half + jnp.dot(e1_ref[:, latent : 2 * latent], sender, preferred_element_type=F32)
     half = half + jnp.dot(e1_ref[:, 2 * latent :], mesh_cols, preferred_element_type=F32)
@@ -230,7 +286,7 @@
     total = parts[0]
     for k in range(1, layers):
         total = total + parts[k]
-    mesh_out_ref[...] = (mesh_ref[...].astype(F32) + total / scale).astype(BF16)
+    mean_ref[...] = total / scale
     for t in range(tiles):
         store(t).wait()
 
@@ -258,44 +314,10 @@
     nodes = mesh_latent.shape[3]
     slots = edge_latent.shape[3]
     layers = lax.axis_size("gz")
-    layer = lax.axis_index("gz")
-    band = lax.axis_index("gx")
-    sector = lax.axis_index("gy")
-    lon_total = lon * lax.axis_size("gy")
     share = slots // layers
+    strip = HALO * lon
     padded = -(-channels // 16) * 16
     tiles = lat // ROWS
-
-    slot_ids = jnp.arange(slots, dtype=jnp.int32)
-    tile = band * lax.axis_size("gy") + sector
-    near = jnp.where(slot_ids < edge_counts[0, 0], receivers[0, 0] - tile * nodes, -1)
-    my_near = lax.dynamic_slice_in_dim(near, layer * share, share)
-    send = lax.dynamic_slice_in_dim(senders[0, 0], layer * share, share)
-    row = send // lon_total - band * lat
-    column = (send % lon_total - sector * lon + HALO + lon_total) % lon_total - HALO
-    above, below = row < 0, row >= lat
-    west, east = column < 0, column >= lon
-    inside_row = ~(above | below)
-    inside_column = ~(west | east)
-    own_index = jnp.where(inside_row & inside_column, row * lon + column, -1)
-    strip = HALO * lon
-    tall = lat * HALO
-    row_index = jnp.where(above, row + HALO, row - lat + HALO) * lon + column
-    beside = jnp.where(west, column + HALO, column - lon)
-    column_index = 2 * strip + jnp.where(west, 0, tall) + row * HALO + beside
-    corner = jnp.where(above, 0, 2) + jnp.where(west, 0, 1)
-    corner_row = jnp.where(above, row + ROWS, row - lat)
-    corner_index = 2 * (strip + tall) + (corner * ROWS + corner_row) * HALO + beside
-    halo_index = jnp.where(
-        inside_column,
-        jnp.where(inside_row, -1, row_index),
-        jnp.where(inside_row, column_index, corner_index),
-    )
-    send_table = jnp.stack([own_index, halo_index, my_near])
-    empty = jnp.zeros_like(embed_b1)
-    vectors = jnp.stack(
-        [embed_b1, embed_gain, edge_b1, message_gain, message_bias, empty, empty, empty]
-    )
 
     vmem = pl.BlockSpec(memory_space=pltpu.VMEM)
     hbm = pl.BlockSpec(memory_space=pl.ANY)
@@ -304,6 +326,12 @@
         ((tiles, padded * ROWS, lon), F32),
         ((latent, padded), BF16),
         ((latent, 8), F32),
+        (edge_w1.shape, BF16),
+        (edge_w2.shape, BF16),
+        ((-(-padded // 128) * 128, latent), F32),
+        ((8, latent), F32),
+        ((1, slots), jnp.int32),
+        ((8, share), jnp.int32),
         ((padded, share), F32),
         ((2, latent, GROUP * lon), F32),
         ((shard * ROWS, lon), F32),
@@ -318,14 +346,17 @@
         ((latent, nodes), F32),
         ((layers, shard, nodes), F32),
     ]
-    sems = [(tiles,), (tiles,), (8,), (8,), (3, layers), (3, layers)]
-    grid_out, mesh_out = pl.pallas_call(
+    sems = [(tiles,), (tiles,), (2,), (8,), (8,), (3, layers), (3, layers)]
+    smem = pl.BlockSpec(memory_space=pltpu.SMEM)
+    line = lambda v: v.reshape(1, v.size)
+    mesh_own = mesh_latent[:, 0, 0, :]
+    grid_out, mean = pl.pallas_call(
         kernel,
-        in_specs=[hbm] + [vmem] * 9,
+        in_specs=[hbm, vmem, vmem, hbm, hbm] + [vmem] * 9 + [smem],
         out_specs=[hbm, vmem],
         out_shape=[
             jax.ShapeDtypeStruct((shard, lat, lon), BF16),
-            jax.ShapeDtypeStruct((shard, nodes), BF16),
+            jax.ShapeDtypeStruct((shard, nodes), F32),
         ],
         scratch_shapes=[pltpu.VMEM(s, d) for s, d in scratch]
         + [pltpu.SemaphoreType.DMA(s) for s in sems],
@@ -333,9 +364,11 @@
             collective_id=0, has_side_effects=True, vmem_limit_bytes=60 * 1024 * 1024
         ),
     )(
-        grid_inputs, embed_w1, embed_w2, edge_w1, edge_w2, vectors,
-        mesh_latent[:, 0, 0, :], edge_latent[:, 0, 0, :], near[None], send_table,
+        grid_inputs, embed_w1.T, embed_w2, edge_w1, edge_w2,
+        line(embed_b1), line(embed_gain), line(edge_b1), line(message_gain), line(message_bias),
+        mesh_own, edge_latent[:, 0, 0, :], line(senders), line(receivers), edge_counts,
     )
+    mesh_out = (mesh_own.astype(F32) + mean).astype(BF16)
     return (mesh_out.reshape(shard, 1, 1, nodes), grid_out)
 
 

time: 56.8 us -> 50.4 us (0.89)
  local copies, waits for them, and re-layouts: 7.7 us -> 3.08 us
  other arithmetic: 2.73 us -> 1.55 us
    unnamed x3, local copies, waits for them, and re-layouts: 6.32 us -> 3.08 us
    select_n x4 -> x0, other arithmetic: 2.12 us -> none  [the longest x2 1.37 us: on_device(): jnp.where(slot_ids < edge_counts[0, 0], receivers[0, 0] - tile * nodes, -1)]
    reshape x0 -> x1, other arithmetic: none -> 1.55 us  [on_device(): return (mesh_out.reshape(shard, 1, 1, nodes), grid_out)]
    another operation x3 -> x0, local copies, waits for them, and re-layouts: 1.38 us -> none  [on_device(): jnp.stack([embed_b1, embed_gain, edge_b1, message_gain, message_bias, emp...]
    another operation x1 -> x0, other arithmetic: 0.61 us -> none  [on_device(): send_table = jnp.stack([own_index, halo_index, my_near])]
where the time goes in v3:
time: 50.4 us; the launch traced here: 49.7 us
  Pallas kernels  43.8 us (87%)
  local copies, waits for them, and re-layouts  3.08 us (6%)
  other arithmetic  1.55 us (3%)
  between operations  1.31 us (3%)
    pallas_call x1, Pallas kernels, on_device(): pl.pallas_call(kernel, in_specs=[hbm, vmem, vmem, hbm, hbm] + [vmem] * 9...  43.8 us
    unnamed x3, local copies, waits for them, and re-layouts  3.08 us
    reshape x1, other arithmetic, on_device(): return (mesh_out.reshape(shard, 1, 1, nodes), grid_out)  1.55 us

profile of v3, /device:TPU:0, one launch (start us, length us, event | category | flops | bytes accessed | tf_op | source)
XLA Modules:
  0.0 49.7 jit_solution(9573093072107779466)
XLA Ops:
  1.3 0.0 copy-start
  1.3 43.8 %shard_map.158 = (bf16[128,64,128]{2,1,0:T(8,128)(2,1)}, f32[128,256]{1,0:T(8,128)}) custom-call(bf16[186,64,128]{2,1,0:T(8,128)(2,1)} %x_hbm.1, bf16[186,512]{1,0:T(8,128)(2,1)} %bitcast.15, bf16[512,512]{1,0:T(8,128)(2,1)} %w2_ref.1, bf16[512,1536]{1,0:T(8,128)(2,1)} %e1_hbm.1, bf16[512,512]{1,0:T(8,128)(2,1)} %e2_hbm.1, f32[1,512]{1,0:T(1,128)} %bitcast.18, ...), custom_call_target="tpu_custom_call" | custom-call | tf_op jit(solution)/shard_map/pallas_call | solution.py:353
  45.1 0.0 copy-done
  45.1 1.5 %fusion = bf16[128,1,1,256]{3,0,2,1:T(8,128)(2,1)} fusion(f32[128,256]{1,0:T(8,128)} %get-tuple-element.4, bf16[128,1,1,256]{3,0,2,1:T(8,128)(2,1)S(1)} %copy-done), kind=kLoop, calls=%fused_computation.1 | loop fusion | flops 98304 | bytes 262144 | tf_op jit(solution)/shard_map/reshape | solution.py:372
  46.7 3.1 %copy.19 = bf16[128,64,128]{2,1,0:T(8,128)(2,1)} copy(bf16[128,64,128]{2,1,0:T(8,128)(2,1)} %get-tuple-element.9) | data formatting | bytes 4194304
Async XLA Ops:
  1.3 43.8 %copy-start = (bf16[128,1,1,256]{3,0,2,1:T(8,128)(2,1)S(1)}, bf16[128,1,1,256]{3,0,2,1:T(8,128)(2,1)}, u32[]{:S(2)}) copy-start(bf16[128,1,1,256]{3,0,2,1:T(8,128)(2,1)} %param.25) | copy-start | bytes 196612
